TPU v7x, 128 devices: a whole 4x4x4 slice. The times are simulated.
128 devices in a mesh: row: 16 (over x, z), col: 8 (over y, core).
Axes of the slice: x: 4, y: 4, z: 4, core: 2. Of those that a mesh axis runs over, the one named last changes fastest.
Arguments:
- basis_blocks: float32 [8, 16, 1048576], P(None, None, ('col', 'row')), may hold values from -6 to 6
- tile_values: bfloat16 [8, 16, 384, 128, 128], P('col', 'row'), may hold values from -0.375 to 0.375
- tile_rows: int32 [8, 16, 384], P('col', 'row'), may hold values from 0 to 1023
- tile_column: int32 [8, 16, 384], P('col', 'row'), may hold values from 0 to 511
- tile_count: int32 [8, 16], P('col', 'row'), may hold values from 1 to 384, as said below
- diagonal: float32 [1048576], P(('col', 'row')), may hold values from 1 to 6
Outputs:
- new_block: float32 [16, 1048576], P(None, ('col', 'row'))
- coefficients: float32 [8, 16, 16], replicated
- triangle: float32 [16, 16], replicated
Inputs may be any that keep to these rules, and one draw needn't show every extreme that they name: Each operator block stores tile_count tiles in its first slots; at most 384, and some block has exactly 384 in every draw. Slots past the count hold arbitrary data and are ignored.
All inputs are finite; a program needn't handle non-finite values.
Results may differ from a plain program's by a relative error of at most 0.0031.
Values may be sent and summed in bfloat16 or wider, within the bound.
A program may use at most 128 MiB of HBM per device.

v0:
```python
import functools

import jax
import jax.numpy as jnp
from jax import lax
from jax.sharding import Mesh
from jax.sharding import PartitionSpec as P

ROW = ("row_0", "row_1")
COL = ("col_0", "col_1")
ROW_COL = ("row_0", "row_1", "col_0", "col_1")
COL_ROW = ("col_0", "col_1", "row_0", "row_1")


def cut_along(shard, dim, length):
    lengths = shard.shape
    parts = shard.reshape(*lengths[:dim], length, lengths[dim] // length, *lengths[dim + 1 :])
    return jnp.moveaxis(parts, dim, 0)


def sum_at_owner(shard, axis, dim):
    parts = cut_along(shard, dim, lax.axis_size(axis))
    arrived = lax.all_to_all(parts, axis, split_axis=0, concat_axis=0, tiled=True)
    return arrived.astype(jnp.float32).sum(axis=0)


def by_axis(shard, axes):
    return functools.reduce(lax.psum, axes, shard)


def gathered_total(shard, axis):
    return lax.all_gather(shard, axis).sum(0)


def local(basis_blocks, tile_values, tile_rows, tile_column, tile_count, diagonal):
    rhs_width = basis_blocks.shape[1]
    seg_rows = basis_blocks.shape[2]
    total_rows = seg_rows * lax.axis_size(ROW) * lax.axis_size(COL)
    block_tiles = lax.axis_size(ROW) * seg_rows // 128
    vector = basis_blocks[-1].astype(jnp.bfloat16)
    expanded = lax.all_gather(vector, COL, axis=1, tiled=True)
    xblocks = expanded.reshape(rhs_width, -1, 128)
    values = tile_values[0, 0]
    row_ids = tile_rows[0, 0]
    column_ids = tile_column[0, 0]
    live_count = tile_count[0, 0]
    live_tiles = jnp.arange(values.shape[0], dtype=jnp.int32) < live_count
    gathered = jnp.take(xblocks, column_ids, axis=1)
    products = jnp.einsum("stj,tji->tsi", gathered, values, preferred_element_type=jnp.float32)
    inside = live_tiles & (row_ids >= 0) & (row_ids < 0 + block_tiles)
    segment_ids = jnp.where(inside, row_ids - 0, block_tiles)
    summed = jax.ops.segment_sum(products, segment_ids, num_segments=block_tiles + 1)
    folded = sum_at_owner(summed[:block_tiles].astype(jnp.bfloat16), ROW, 0)
    image_rows = folded.transpose(1, 0, 2).reshape(rhs_width, seg_rows)
    image_rows = image_rows + diagonal[None, :] * basis_blocks[-1]
    highest = lax.Precision.HIGHEST
    local_proj = jnp.einsum("kap,bp->kab", basis_blocks, image_rows, precision=highest)
    coefficients = by_axis(local_proj, ROW_COL) / total_rows
    projected = image_rows - jnp.einsum(
        "kab,kap->bp", coefficients, basis_blocks, precision=highest
    )
    local_gram = jnp.dot(projected, projected.T, precision=highest)
    gram_matrix = gathered_total(local_gram, ROW_COL) / total_rows
    lower_factor = jnp.linalg.cholesky(gram_matrix)
    new_block = lax.linalg.triangular_solve(lower_factor, projected, left_side=True, lower=True)
    return (new_block, coefficients, lower_factor.T)


def solution(mesh):
    split = Mesh(mesh.devices.reshape(4, 4, 4, 2), ("row_0", "row_1", "col_0", "col_1"))
    placed = (
        P(None, None, COL_ROW),
        P(COL, ROW, None, None, None),
        P(COL, ROW, None),
        P(COL, ROW, None),
        P(COL, ROW),
        P(COL_ROW),
    )
    return jax.shard_map(
        local, mesh=split, in_specs=placed, out_specs=(P(None, COL_ROW), P(), P()), check_vma=False
    )
```

profile of v0, /device:TPU:1, one launch (start us, length us, event | category | flops | bytes accessed | tf_op | source)
XLA Modules:
  0.0 291.3 jit_solution(7420172091510174178)
XLA Ops:
  7.2 0.0 all-gather.3.cloned.1.call-start
  7.2 1.8 bitcast_convert_fusion
  9.0 0.0 all-gather.3.cloned.1.call-update
  9.7 0.7 reduce.7
  10.4 0.7 fusion.12
  11.1 0.7 fusion.13
  11.8 27.4 %all-gather.3.cloned.1.call-done = bf16[16,65536]{1,0:T(8,128)(2,1)} async-done(((bf16[16,8192]{1,0:T(8,128)(2,1)}), bf16[16,65536]{1,0:T(8,128)(2,1)}) %all-gather.3.cloned.1.call-update) | async-done | bytes 2097168 | tf_op jit(solution)/shard_map/all_gather | solution.py:41
  39.2 2.0 copy_bitcast_fusion
  41.1 2.6 gather_fusion
  43.7 6.9 %fusion = f32[384,16,128]{2,1,0:T(8,128)S(1)} fusion(bf16[1,1,384,128,128]{4,3,2,1,0:T(8,128)(2,1)} %param.7, bf16[384,16,128]{2,1,0:T(8,128)(2,1)} %gather_fusion, pred[384]{0:T(512)(128)(4,1)S(1)} %compare_and_fusion), kind=kOutput, calls=%fused_computation.2 | convolution fusion | flops 202113024 | bytes 17301888 | tf_op jit(solution)/shard_map/stj,tji->tsi/dot_general | solution.py:49
  50.6 3.5 %broadcast_in_dim.19 = f32[1025,16,128]{2,1,0:T(8,128)} broadcast(f32[]{:T(128)} %constant.59.clone.1), dimensions={} | broadcast | bytes 8396804 | tf_op jit(solution)/shard_map/broadcast_in_dim | solution.py:52
  54.1 49.0 %scatter_fusion = f32[1025,16,128]{2,1,0:T(8,128)} fusion(f32[1025,16,128]{2,1,0:T(8,128)} %broadcast_in_dim.19, s32[384]{0:T(512)S(1)} %fusion.13, f32[384,16,128]{2,1,0:T(8,128)S(1)} %fusion), kind=kCustom, calls=%fused_computation.1 | custom fusion | flops 786432 | bytes 9438720 | tf_op jit(solution)/shard_map/scatter-add | solution.py:52
  103.0 3.9 %slice.31 = bf16[1024,16,128]{2,1,0:T(8,128)(2,1)S(1)} slice(f32[1025,16,128]{2,1,0:T(8,128)} %scatter_fusion), slice={[0:1024], [0:16], [0:128]} | slice | bytes 8388608 | tf_op jit(solution)/shard_map/slice | solution.py:53
  107.0 58.8 %all_to_all.5 = bf16[16,64,16,128]{3,2,1,0:T(8,128)(2,1)S(1)} all-to-all(bf16[16,64,16,128]{3,2,1,0:T(8,128)(2,1)S(1)} %bitcast.70), channel_id=1, replica_groups=mesh['row_0'=4,'row_1'=4,'col_0'=4,'col_1'=2] {'row_0','row_1'}, dimensions={0} | all-to-all | bytes 8388608 | tf_op jit(solution)/shard_map/all_to_all | solution.py:23
  165.7 0.0 copy-start
  165.7 0.0 copy-start.1
  165.7 0.6 convert_reduce_fusion
  166.3 1.6 copy-done
  167.9 0.0 copy-done.1
  167.9 14.7 %convolution_bitcast_fusion.1 = f32[8,16,16]{1,2,0:T(8,128)S(1)} fusion(f32[8,16,8192]{2,1,0:T(8,128)S(1)} %copy-done, f32[8192]{0:T(1024)S(1)} %copy-done.1, f32[64,16,128]{2,1,0:T(8,128)S(1)} %convert_reduce_fusion), kind=kOutput, calls=%fused_computation.12 | convolution fusion | flops 201588736 | bytes 5283840 | tf_op jit(solution)/shard_map/kap,bp->kab/dot_general | solution.py:57
  182.6 12.4 %psum.28 = f32[8,16,16]{1,2,0:T(8,128)S(1)} all-reduce(f32[8,16,16]{1,2,0:T(8,128)S(1)} %convolution_bitcast_fusion.1), channel_id=1, replica_groups=mesh['row_0'=4,'row_1'=4,'col_0'=4,'col_1'=2] {'row_0'}, use_global_device_ids=true, to_apply=%region_2.3 | all-reduce | flops 2048 | bytes 16384 | tf_op jit(solution)/shard_map/psum | solution.py:28
  195.0 12.0 %psum.29 = f32[8,16,16]{1,2,0:T(8,128)S(1)} all-reduce(f32[8,16,16]{1,2,0:T(8,128)S(1)} %psum.28), channel_id=1, replica_groups=mesh['row_0'=4,'row_1'=4,'col_0'=4,'col_1'=2] {'row_1'}, use_global_device_ids=true, to_apply=%region_3.4 | all-reduce | flops 2048 | bytes 16384 | tf_op jit(solution)/shard_map/psum | solution.py:28
  207.0 12.3 %psum.30 = f32[8,16,16]{1,2,0:T(8,128)S(1)} all-reduce(f32[8,16,16]{1,2,0:T(8,128)S(1)} %psum.29), channel_id=1, replica_groups=mesh['row_0'=4,'row_1'=4,'col_0'=4,'col_1'=2] {'col_0'}, use_global_device_ids=true, to_apply=%region_4.5 | all-reduce | flops 2048 | bytes 16384 | tf_op jit(solution)/shard_map/psum | solution.py:28
  219.4 16.2 %psum.31 = f32[8,16,16]{1,2,0:T(8,128)S(1)} all-reduce(f32[8,16,16]{1,2,0:T(8,128)S(1)} %psum.30), channel_id=1, replica_groups=mesh['row_0'=4,'row_1'=4,'col_0'=4,'col_1'=2] {'col_1'}, use_global_device_ids=true, to_apply=%region_5.6 | all-reduce | flops 2048 | bytes 16384 | tf_op jit(solution)/shard_map/psum | solution.py:28
  235.6 6.7 %fusion.2 = f32[16,8192]{1,0:T(8,128)S(1)} fusion(f32[8,16,8192]{2,1,0:T(8,128)} %param.6, f32[8192]{0:T(1024)S(1)} %copy-done.1, f32[8,16,16]{1,2,0:T(8,128)S(1)} %psum.31, f32[64,16,128]{2,1,0:T(8,128)S(1)} %convert_reduce_fusion), kind=kOutput, calls=%fused_computation.5 | convolution fusion | flops 201721856 | bytes 5808128 | tf_op jit(solution)/shard_map/kab,kap->bp/dot_general | solution.py:59
  242.4 0.7 copy.23
  243.1 0.8 fusion.15
  243.9 34.2 %all-gather = f32[2048,16]{1,0:T(8,128)S(1)} all-gather(f32[16,16]{1,0:T(8,128)S(1)} %fusion.15), channel_id=2, replica_groups=mesh['row_0'=4,'row_1'=4,'col_0'=4,'col_1'=2] {'row_0','row_1','col_0','..., dimensions={0}, use_global_device_ids=true | all-gather | bytes 132096 | tf_op jit(solution)/shard_map/all_gather | solution.py:32
  278.1 0.1 reduce_sum.21
  278.2 0.1 copy.22
  278.3 1.5 cholesky.16
  279.8 0.6 compare_reduce_fusion
  280.4 0.6 fusion.11
  281.1 0.7 copy.24
  281.7 1.2 custom-call.6
  283.0 1.4 fusion.8
  (5 shorter events, 0.1 us)
Async XLA Ops:
  7.2 32.0 %all-gather.3.cloned.1.call-start = ((), (), s32[]{:S(2)}) async-start(), calls=%async_computation.1 | async-start | bytes 2359296 | tf_op jit(solution)/shard_map/all_gather | solution.py:41
  165.7 2.2 copy-start
  165.7 2.2 copy-start.1
Sparse Core Ops, SparseCore 0:
  10.2 28.8 all-gather.2
where the time goes:
time: 293 us; the launch traced here: 291 us
  blocking collectives  146 us (50%)
  other arithmetic  55.8 us (19%)
  matrix products  30.5 us (10%)
  waiting for transfers between devices  27.4 us (9%)
  local copies, waits for them, and re-layouts  16.8 us (6%)
  between operations  14.8 us (5%)
    all_to_all x1, blocking collectives, sum_at_owner(): lax.all_to_all(parts, axis, split_axis=0, concat_axis=0, tiled=True)  58.8 us
    psum x4, blocking collectives, by_axis(): return functools.reduce(lax.psum, axes, shard)  53 us
    scatter-add x1, other arithmetic, local(): jax.ops.segment_sum(products, segment_ids, num_segments=block_tiles + 1)  49 us
    all_gather x1, blocking collectives, gathered_total(): return lax.all_gather(shard, axis).sum(0)  34.2 us
    all_gather x1, waiting for transfers between devices, local(): expanded = lax.all_gather(vector, COL, axis=1, tiled=True)  27.4 us
    dot_general x1, matrix products, local(): jnp.einsum('kap,bp->kab', basis_blocks, image_rows, precision=highest)  14.7 us
    dot_general x1, matrix products, local(): jnp.einsum('stj,tji->tsi', gathered, values, preferred_element_type=jnp.f...  6.87 us
    dot_general x1, matrix products, local(): jnp.einsum('kab,kap->bp', coefficients, basis_blocks, precision=highest)  6.75 us
  transfers between devices with their start and end apart: 1, of which 1 were waited for; matrix products, arithmetic and copies ran while one was open for 1% of the time, Pallas kernels for 0%

commit v1 on v0

v1 whole, which is shorter than its diff:
```python
import functools

import jax
import jax.numpy as jnp
from jax import lax
from jax.experimental import pallas as pl
from jax.experimental.pallas import tpu as pltpu
from jax.sharding import Mesh
from jax.sharding import PartitionSpec as P

X, Z, Y, K = "row_0", "row_1", "col_0", "col_1"
ROW = (X, Z)
COL = (Y, K)
COL_ROW = (Y, K, X, Z)
MESH = pl.DeviceIdType.MESH
F32, BF16 = jnp.float32, jnp.bfloat16
NT = (((1,), (1,)), ((), ()))
CHUNK = 1024


def send(src, dst, send_sem, recv_sem, **to):
    return pltpu.make_async_remote_copy(
        src_ref=src, dst_ref=dst, send_sem=send_sem, recv_sem=recv_sem, device_id=to, device_id_type=MESH
    )


def halves(value):
    high = value.astype(BF16)
    return high, (value - high.astype(F32)).astype(BF16)


def dot(a, b, dims=(((1,), (0,)), ((), ()))):
    return lax.dot_general(a, b, dims, preferred_element_type=F32)


def lanes(m):
    return pl.ds(pl.multiple_of(m * 128, 128), 128)


def kernel(
    total_rows,
    cols_ref, prev_ref, last_ref, basis_hbm, tiles_hbm, diag_ref,
    out_ref, coef_ref, tri_ref,
    basis, tiles, xg, chain, qh, ql, w,
    sb1, rb1, sb2, rb2, zside, zown,
    inner, outer,
    load_sem, ag_send, ag_recv, rs_send, rs_recv, ar_send, ar_recv,
):
    x0, z0, y0, k0 = (lax.axis_index(a) for a in (X, Z, Y, K))
    blocks, rhs, seg = basis.shape
    slots = tiles.shape[0]
    seg_tiles = seg // 128
    part = seg_tiles // 2
    quarter = part // 2
    c0 = y0 * 2 + k0
    r0 = x0 * 4 + z0

    load_vector = pltpu.make_async_copy(basis_hbm.at[blocks - 1], basis.at[blocks - 1], load_sem.at[0])
    load_basis = pltpu.make_async_copy(
        basis_hbm.at[pl.ds(0, blocks - 1)], basis.at[pl.ds(0, blocks - 1)], load_sem.at[1]
    )
    load_vector.start()
    load_basis.start()
    piece = slots // 4
    loads = [
        pltpu.make_async_copy(
            tiles_hbm.at[pl.ds(i * piece, piece)], tiles.at[pl.ds(i * piece, piece)], load_sem.at[2 + i]
        )
        for i in range(4)
    ]
    for copy in loads:
        copy.start()

    barrier = pltpu.get_barrier_semaphore()
    inner_peers = [lax.rem(c0 + d, 8) for d in range(1, 8)]
    outer_peers = [lax.rem(r0 + d, 16) for d in range(1, 16)]
    for p in inner_peers:
        pl.semaphore_signal(barrier, inc=1, device_id={Y: p // 2, K: lax.rem(p, 2)}, device_id_type=MESH)
    for p in outer_peers:
        pl.semaphore_signal(barrier, inc=1, device_id={X: p // 4, Z: lax.rem(p, 4)}, device_id_type=MESH)

    load_vector.wait()
    own = c0 * seg_tiles

    def to_tiles(m, _):
        xg[own + m] = basis[blocks - 1, :, lanes(m)].astype(BF16)
        return 0

    lax.fori_loop(0, seg_tiles, to_tiles, 0, unroll=8)
    pl.semaphore_wait(barrier, 22)

    up, down, far = lax.rem(y0 + 1, 4), lax.rem(y0 + 3, 4), lax.rem(y0 + 2, 4)

    def chunk(y, k, h):
        return xg.at[pl.ds((y * 2 + k) * seg_tiles + h * part, part)]

    def hop(i, y, h, to):
        ref = chunk(y, k0, h)
        return send(ref, ref, ag_send.at[i], ag_recv.at[i], **{Y: to})

    def across(i, y, h, k):
        ref = chunk(y, k, h)
        return send(ref, ref, ag_send.at[6 + i], ag_recv.at[6 + i], **{K: 1 - k0})

    hops = [hop(0, y0, 0, up), hop(1, y0, 1, up), hop(2, y0, 1, down), hop(3, y0, 0, down)]
    for i in (0, 2, 1, 3):
        hops[i].start()
    arrive = [
        hop(0, down, 0, up), hop(1, down, 1, up), hop(2, up, 1, down),
        hop(3, up, 0, down), hop(4, far, 0, up), hop(5, far, 1, down),
    ]
    over = [across(i * 2 + h, y, h, k0) for i, y in enumerate((y0, down, up, far)) for h in range(2)]
    over[0].start()
    over[1].start()

    load_basis.wait()

    def split_basis(i, _):
        at = pl.ds(pl.multiple_of(i * CHUNK, CHUNK), CHUNK)
        for k in range(blocks):
            high, low = halves(basis[k, :, at])
            qh[pl.ds(k * rhs, rhs), at] = high
            ql[pl.ds(k * rhs, rhs), at] = low
        w[:, at] = basis[blocks - 1, :, at] * diag_ref[:, at]
        return 0

    lax.fori_loop(0, seg // CHUNK, split_basis, 0)

    arrive[0].wait_recv()
    forward_up = hop(4, down, 0, up)
    forward_up.start()
    over[2].start()
    arrive[2].wait_recv()
    forward_down = hop(5, up, 1, down)
    forward_down.start()
    over[5].start()
    for i, j in ((1, 3), (3, 4), (4, 6), (5, 7)):
        arrive[i].wait_recv()
        over[j].start()
    for i, y in enumerate((y0, down, up, far)):
        for h in range(2):
            across(i * 2 + h, y, h, 1 - k0).wait_recv()
    for copy in loads:
        copy.wait()

    chain[0] = jnp.zeros((rhs, 128), F32)
    step = 16

    def products(i, _):
        base = i * step
        made = [dot(xg[cols_ref[base + j]], tiles[base + j]) for j in range(step)]
        for j in range(step):
            chain[base + j + 1] = made[j] + chain[prev_ref[base + j]]
        return 0

    lax.fori_loop(0, slots // step, products, 0)

    for copy in hops + over + [forward_up, forward_down]:
        copy.wait_send()

    first = ((X, x0), (Z, z0))
    second = ((Z, z0), (X, x0))

    def near(pos, d):
        return lax.rem(pos + d, 4)

    def partial(half, f, g, m):
        r = f * 4 + g if half == 0 else g * 4 + f
        return chain[last_ref[r * seg_tiles + half * part + m]]

    def hop1(half, i):
        axis, pos = first[half]
        return send(
            sb1.at[half, i], rb1.at[half, i], rs_send.at[half, i], rs_recv.at[half, i],
            **{axis: near(pos, 1 if i % 2 == 0 else 3)},
        )

    def hop2(half, i):
        axis, pos = second[half]
        return send(
            sb2.at[half, i], rb2.at[half, i], rs_send.at[half, 6 + i], rs_recv.at[half, 6 + i],
            **{axis: near(pos, 1 if i % 2 == 0 else 3)},
        )

    def fill1(half, i, f, h, arrived=None):
        def body(m, _):
            for g in range(2):
                value = partial(half, f, 2 * h + g, m)
                if arrived is not None:
                    value = value + rb1[half, arrived, g * part + m].astype(F32)
                sb1[half, i, g * part + m] = value.astype(BF16)
            return 0

        lax.fori_loop(0, part, body, 0, unroll=8)
        hop1(half, i).start()

    for half in range(2):
        f0 = first[half][1]
        fill1(half, 0, near(f0, 2), 0)
        fill1(half, 1, near(f0, 2), 1)
    for half in range(2):
        f0 = first[half][1]
        fill1(half, 2, near(f0, 1), 1)
        fill1(half, 3, near(f0, 3), 0)
    for half in range(2):
        f0 = first[half][1]
        hop1(half, 0).wait_recv()
        fill1(half, 4, near(f0, 1), 0, 0)
        hop1(half, 1).wait_recv()
        fill1(half, 5, near(f0, 3), 1, 1)

    def summed1(half, g, m):
        h = g // 2
        at = (g - 2 * h) * part + m
        return (
            partial(half, first[half][1], g, m)
            + rb1[half, 3 - h, at].astype(F32)
            + rb1[half, 4 + h, at].astype(F32)
        )

    def over_part(body):
        lax.fori_loop(0, quarter, lambda m, _: (body(m), 0)[1], 0, unroll=8)

    for half in range(2):
        g0 = second[half][1]
        for i in range(2, 6):
            hop1(half, i).wait_recv()

        def far_block(m):
            sb2[half, 0, m] = summed1(half, near(g0, 2), m).astype(BF16)
            sb2[half, 1, m] = summed1(half, near(g0, 2), quarter + m).astype(BF16)

        over_part(far_block)
        hop2(half, 0).start()
        hop2(half, 1).start()

        def near_block(m):
            sb2[half, 2, m] = summed1(half, near(g0, 1), quarter + m).astype(BF16)
            sb2[half, 3, m] = summed1(half, near(g0, 3), m).astype(BF16)

        over_part(near_block)
        hop2(half, 2).start()
        hop2(half, 3).start()

        def kept(m):
            zside[half, 0, m] = summed1(half, near(g0, 1), m)
            zside[half, 1, m] = summed1(half, near(g0, 3), quarter + m)
            zown[half, m] = summed1(half, g0, m)
            zown[half, quarter + m] = summed1(half, g0, quarter + m)

        over_part(kept)
    for half in range(2):
        hop2(half, 0).wait_recv()
        hop2(half, 1).wait_recv()

        def joined(m):
            sb2[half, 4, m] = (zside[half, 0, m] + rb2[half, 0, m].astype(F32)).astype(BF16)
            sb2[half, 5, m] = (zside[half, 1, m] + rb2[half, 1, m].astype(F32)).astype(BF16)

        over_part(joined)
        hop2(half, 4).start()
        hop2(half, 5).start()
    for half in range(2):
        for i in range(2, 6):
            hop2(half, i).wait_recv()

        def arrived_rows(m):
            low = lanes(half * part + m)
            w[:, low] = w[:, low] + (
                zown[half, m] + rb2[half, 3, m].astype(F32) + rb2[half, 4, m].astype(F32)
            )
            high = lanes(half * part + quarter + m)
            w[:, high] = w[:, high] + (
                zown[half, quarter + m] + rb2[half, 2, m].astype(F32) + rb2[half, 5, m].astype(F32)
            )

        over_part(arrived_rows)

    def total(value, use):
        def inner_copy(d):
            p = lax.rem(c0 + d, 8)
            mine = inner.at[use, c0]
            return send(
                mine, mine, ar_send.at[use, d], ar_recv.at[use, d], **{Y: p // 2, K: lax.rem(p, 2)}
            )

        def outer_copy(d):
            p = lax.rem(r0 + d, 16)
            mine = outer.at[use, r0]
            return send(
                mine, mine, ar_send.at[use, 8 + d], ar_recv.at[use, 8 + d], **{X: p // 4, Z: lax.rem(p, 4)}
            )

        inner[use, c0] = value
        for d in range(1, 8):
            inner_copy(d).start()
        for d in range(1, 8):
            inner_copy(d).wait_recv()
        acc = inner[use, 0]
        for i in range(1, 8):
            acc = acc + inner[use, i]
        outer[use, r0] = acc
        for d in range(1, 16):
            outer_copy(d).start()
        for d in range(1, 16):
            outer_copy(d).wait_recv()
        acc = outer[use, 0]
        for i in range(1, 16):
            acc = acc + outer[use, i]
        for d in range(1, 8):
            inner_copy(d).wait_send()
        for d in range(1, 16):
            outer_copy(d).wait_send()
        return acc * F32(1.0 / total_rows)

    def project(i, acc):
        at = pl.ds(pl.multiple_of(i * CHUNK, CHUNK), CHUNK)
        high, low = halves(w[:, at])
        both = dot(jnp.concatenate([high, low], axis=0), qh[:, at], NT)
        return acc + (both[:rhs] + both[rhs:] + dot(high, ql[:, at], NT))

    coef = total(lax.fori_loop(0, seg // CHUNK, project, jnp.zeros((rhs, blocks * rhs), F32)), 0)
    coef_ref[...] = coef
    coef_high, coef_low = halves(coef)
    coef_both = jnp.concatenate([coef_high, coef_low], axis=0)

    def subtract(i, acc):
        at = pl.ds(pl.multiple_of(i * CHUNK, CHUNK), CHUNK)
        both = dot(coef_both, qh[:, at])
        rest = w[:, at] - (both[:rhs] + both[rhs:] + dot(coef_high, ql[:, at]))
        w[:, at] = rest
        high, low = halves(rest)
        both = dot(jnp.concatenate([high, low], axis=0), high, NT)
        return acc + (both[:rhs] + both[rhs:] + dot(high, low, NT))

    gram = lax.fori_loop(0, seg // CHUNK, subtract, jnp.zeros((rhs, rhs), F32))
    gram = total(jnp.concatenate([gram, jnp.zeros((rhs, 128 - rhs), F32)], axis=1), 1)

    row = lax.broadcasted_iota(jnp.int32, (rhs, 128), 0)
    lane = lax.broadcasted_iota(jnp.int32, (rhs, 128), 1)
    m = jnp.where(lane < rhs, gram, jnp.where(lane - rhs == row, F32(1), F32(0)))
    for k in range(rhs - 1):
        factor = jnp.where(row[:, :1] > k, m[:, k : k + 1] / m[k : k + 1, k : k + 1], F32(0))
        m = m - factor * m[k : k + 1, :]
    pivots = jnp.sum(jnp.where(lane == row, m, F32(0)), axis=1, keepdims=True)
    m = m / jnp.sqrt(pivots)
    tri_ref[...] = jnp.where(lane >= row, m, F32(0))[:, :rhs]
    inv_high, inv_low = halves(m[:, rhs : 2 * rhs])
    inv_both = jnp.concatenate([inv_high, inv_low], axis=0)

    def solve(i, _):
        at = pl.ds(pl.multiple_of(i * CHUNK, CHUNK), CHUNK)
        high, low = halves(w[:, at])
        both = dot(inv_both, high)
        out_ref[:, at] = both[:rhs] + both[rhs:] + dot(inv_high, low)
        return 0

    lax.fori_loop(0, seg // CHUNK, solve, 0)
    for half in range(2):
        for i in range(6):
            hop1(half, i).wait_send()
            hop2(half, i).wait_send()


def local(basis_blocks, tile_values, tile_rows, tile_column, tile_count, diagonal):
    blocks, rhs, seg = basis_blocks.shape
    slots = tile_values.shape[2]
    seg_tiles = seg // 128
    part = seg_tiles // 2
    total_rows = seg * 128
    block_tiles = seg_tiles * 16

    slot = jnp.arange(slots, dtype=jnp.int32)
    live = slot < tile_count[0, 0]
    rows = jnp.where(live, tile_rows[0, 0], -1)
    cols = jnp.where(live, tile_column[0, 0], 0)
    earlier = (rows[:, None] == rows[None, :]) & (slot[:, None] < slot[None, :])
    prev = jnp.max(jnp.where(earlier, slot[:, None] + 1, 0), axis=0)
    hit = rows[:, None] == jnp.arange(block_tiles, dtype=jnp.int32)[None, :]
    last = jnp.max(jnp.where(hit, slot[:, None] + 1, 0), axis=0)

    smem = pl.BlockSpec(memory_space=pltpu.SMEM)
    vmem = pl.BlockSpec(memory_space=pltpu.VMEM)
    hbm = pl.BlockSpec(memory_space=pl.ANY)
    dma = pltpu.SemaphoreType.DMA
    tile = (rhs, 128)
    new_block, coef, triangle = pl.pallas_call(
        functools.partial(kernel, total_rows),
        out_shape=(
            jax.ShapeDtypeStruct((rhs, seg), F32),
            jax.ShapeDtypeStruct((rhs, blocks * rhs), F32),
            jax.ShapeDtypeStruct((rhs, rhs), F32),
        ),
        in_specs=[smem, smem, smem, hbm, hbm, vmem],
        out_specs=(vmem, vmem, vmem),
        scratch_shapes=[
            pltpu.VMEM((blocks, rhs, seg), F32),
            pltpu.VMEM((slots, 128, 128), BF16),
            pltpu.VMEM((8 * seg_tiles, *tile), BF16),
            pltpu.VMEM((slots + 8, *tile), F32),
            pltpu.VMEM((blocks * rhs, seg), BF16),
            pltpu.VMEM((blocks * rhs, seg), BF16),
            pltpu.VMEM((rhs, seg), F32),
            pltpu.VMEM((2, 6, 2 * part, *tile), BF16),
            pltpu.VMEM((2, 6, 2 * part, *tile), BF16),
            pltpu.VMEM((2, 6, part // 2, *tile), BF16),
            pltpu.VMEM((2, 6, part // 2, *tile), BF16),
            pltpu.VMEM((2, 2, part // 2, *tile), F32),
            pltpu.VMEM((2, part, *tile), F32),
            pltpu.VMEM((2, 8, *tile), F32),
            pltpu.VMEM((2, 16, *tile), F32),
            dma((6,)),
            dma((14,)),
            dma((14,)),
            dma((2, 12)),
            dma((2, 12)),
            dma((2, 24)),
            dma((2, 24)),
        ],
        compiler_params=pltpu.CompilerParams(
            collective_id=0, has_side_effects=True, vmem_limit_bytes=58 * 1024 * 1024
        ),
        name="step",
    )(cols, prev, last, basis_blocks, tile_values[0, 0], diagonal[None, :])
    return new_block, coef.T.reshape(blocks, rhs, rhs), triangle


def solution(mesh):
    split = Mesh(mesh.devices.reshape(4, 4, 4, 2), (X, Z, Y, K))
    placed = (
        P(None, None, COL_ROW),
        P(COL, ROW, None, None, None),
        P(COL, ROW, None),
        P(COL, ROW, None),
        P(COL, ROW),
        P(COL_ROW),
    )
    return jax.shard_map(
        local, mesh=split, in_specs=placed, out_specs=(P(None, COL_ROW), P(), P()), check_vma=False
    )
```

time: 293 us -> 91.7 us (0.31)
  blocking collectives: 146 us -> 0 us
  Pallas kernels: 0 us -> 81.9 us
  other arithmetic: 55.8 us -> 3.63 us
  matrix products: 30.5 us -> 0 us
  waiting for transfers between devices: 27.4 us -> 0 us
  between operations: 14.8 us -> 1.3 us
  local copies, waits for them, and re-layouts: 16.8 us -> 4.59 us
    pallas_call x0 -> x1, Pallas kernels: none -> 81.9 us  [local(): pl.pallas_call(functools.partial(kernel, total_rows), out_shape=(jax.Shap...]
    all_to_all x1 -> x0, blocking collectives: 58.8 us -> none  [sum_at_owner(): lax.all_to_all(parts, axis, split_axis=0, concat_axis=0, tiled=True)]
    psum x4 -> x0, blocking collectives: 53 us -> none  [by_axis(): return functools.reduce(lax.psum, axes, shard)]
    scatter-add x1 -> x0, other arithmetic: 49 us -> none  [local(): jax.ops.segment_sum(products, segment_ids, num_segments=block_tiles + 1)]
    all_gather x1 -> x0, blocking collectives: 34.2 us -> none  [gathered_total(): return lax.all_gather(shard, axis).sum(0)]
    dot_general x4 -> x0, matrix products: 29.1 us -> none  [the longest x1 14.7 us: local(): jnp.einsum('kap,bp->kab', basis_blocks, image_rows, precision=highest)]
    all_gather x1 -> x0, waiting for transfers between devices: 27.4 us -> none  [local(): expanded = lax.all_gather(vector, COL, axis=1, tiled=True)]
    slice x1 -> x0, local copies, waits for them, and re-layouts: 3.92 us -> none  [local(): folded = sum_at_owner(summed[:block_tiles].astype(jnp.bfloat16), ROW, 0)]
  transfers between devices with their start and end apart: 1 -> 0, of which waited for: 1 -> 0; matrix products, arithmetic and copies ran while one was open for 1% -> 0% of each run, Pallas kernels for 0% -> 0%
where the time goes in v1:
time: 91.7 us; the launch traced here: 91.4 us
  Pallas kernels  81.9 us (89%)
  local copies, waits for them, and re-layouts  4.59 us (5%)
  other arithmetic  3.63 us (4%)
  between operations  1.3 us (1%)
    pallas_call x1, Pallas kernels, local(): pl.pallas_call(functools.partial(kernel, total_rows), out_shape=(jax.Shap...  81.9 us
    unnamed x3, local copies, waits for them, and re-layouts  4.59 us

profile of v1, /device:TPU:1, one launch (start us, length us, event | category | flops | bytes accessed | tf_op | source)
XLA Modules:
  0.0 91.4 jit_solution(2213943941459769471)
XLA Ops:
  1.3 0.7 reduce.1
  2.0 0.7 reduce
  2.7 0.6 fusion.1
  3.3 0.8 select_reduce_fusion.1.prev_ref
  4.0 0.9 select_reduce_fusion.last_ref
  4.9 81.9 %step.1 = (f32[16,8192]{1,0:T(8,128)}, f32[16,128]{1,0:T(8,128)}, f32[16,16]{1,0:T(8,128)}) custom-call(s32[384]{0:T(512)} %get-tuple-element.16.cols_ref, s32[384]{0:T(512)} %select_reduce_fusion.1.prev_ref, s32[1024]{0:T(1024)} %select_reduce_fusion.last_ref, f32[8,16,8192]{2,1,0:T(8,128)} %basis_hbm.1, bf16[384,128,128]{2,1,0:T(8,128)(2,1)} %bitcast.6, ...), custom_call_target="tpu_custom_call" | custom-call | tf_op jit(solution)/shard_map/step/pallas_call | solution.py:387
  86.8 1.4 %copy.11 = f32[128,16]{1,0:T(8,128)} copy(f32[128,16]{0,1:T(8,128)} %bitcast.9) | data formatting | bytes 16384
  88.2 1.9 %copy.15 = f32[16,8192]{1,0:T(8,128)} copy(f32[16,8192]{1,0:T(8,128)} %get-tuple-element.20) | data formatting | bytes 1048576
  90.1 1.3 %copy.16 = f32[16,16]{1,0:T(8,128)} copy(f32[16,16]{1,0:T(8,128)} %get-tuple-element.22) | data formatting | bytes 2048
  (1 shorter events, 0.0 us)

commit v2 on v1

--- a/solution.py
+++ b/solution.py
@@ -39,12 +39,13 @@
 
 def kernel(
     total_rows,
-    cols_ref, prev_ref, last_ref, basis_hbm, tiles_hbm, diag_ref,
+    count_ref, cols_ref, rows_ref, basis_hbm, tiles_hbm, diag_ref,
     out_ref, coef_ref, tri_ref,
-    basis, tiles, xg, chain, qh, ql, w,
+    basis, tiles, xg, chain, q2, w,
     sb1, rb1, sb2, rb2, zside, zown,
-    inner, outer,
-    load_sem, ag_send, ag_recv, rs_send, rs_recv, ar_send, ar_recv,
+    prev_vec, last_vec, prev_ref, last_ref,
+    mine, pair, ring, whole, inner, outer,
+    load_sem, ag_send, ag_recv, rs_send, rs_recv, ea_send, ea_recv, ar_send, ar_recv,
 ):
     x0, z0, y0, k0 = (lax.axis_index(a) for a in (X, Z, Y, K))
     blocks, rhs, seg = basis.shape
@@ -115,32 +116,97 @@
 
     load_basis.wait()
 
-    def split_basis(i, _):
+    width = blocks * rhs
+
+    def split_basis(i, acc):
         at = pl.ds(pl.multiple_of(i * CHUNK, CHUNK), CHUNK)
         for k in range(blocks):
             high, low = halves(basis[k, :, at])
-            qh[pl.ds(k * rhs, rhs), at] = high
-            ql[pl.ds(k * rhs, rhs), at] = low
-        w[:, at] = basis[blocks - 1, :, at] * diag_ref[:, at]
-        return 0
-
-    lax.fori_loop(0, seg // CHUNK, split_basis, 0)
+            q2[pl.ds(k * rhs, rhs), at] = high
+            q2[pl.ds(width + k * rhs, rhs), at] = low
+        shifted = basis[blocks - 1, :, at] * diag_ref[:, at]
+        w[:, at] = shifted
+        stack = jnp.concatenate([q2[:, at], shifted.astype(BF16)], axis=0)
+        return acc + dot(stack, q2[pl.ds(0, width), at], NT)
+
+    made = lax.fori_loop(0, seg // CHUNK, split_basis, jnp.zeros((2 * width + rhs, width), F32))
+    mine[pl.ds(0, width)] = made[:width] + made[width : 2 * width] + made[width : 2 * width].T
+    mine[pl.ds(width, rhs)] = made[2 * width :]
+
+    load = (width + rhs) // 2
+    ring_axes = ((X, x0), (Z, z0), (Y, y0))
+    to_pair = send(
+        mine.at[pl.ds(pl.multiple_of((1 - k0) * load, 8), load)], pair, ea_send.at[0], ea_recv.at[0], **{K: 1 - k0}
+    )
+    to_pair.start()
+
+    def ring_copy(i, d):
+        axis, pos = ring_axes[i]
+        ref = ring.at[i, pos]
+        return send(ref, ref, ea_send.at[3 * i + d], ea_recv.at[3 * i + d], **{axis: lax.rem(pos + d, 4)})
+
+    def ring_start(i, value):
+        ring[i, ring_axes[i][1]] = value
+        for d in range(1, 4):
+            ring_copy(i, d).start()
+
+    def ring_sum(i):
+        for d in range(1, 4):
+            ring_copy(i, d).wait_recv()
+        return (ring[i, 0] + ring[i, 1]) + (ring[i, 2] + ring[i, 3])
+
+    lane_slot = lax.broadcasted_iota(jnp.int32, (1, 128), 1)
+    sub_slot = lax.broadcasted_iota(jnp.int32, (128, 128), 0)
+    count = count_ref[0, 0]
+    row_lanes, row_subs = [], []
+    for c in range(slots // 128):
+        row_c = rows_ref[:, pl.ds(c * 128, 128)]
+        row_c = jnp.where(lane_slot + c * 128 < count, row_c, -1)
+        row_lanes.append(row_c)
+        row_subs.append(jnp.broadcast_to(row_c, (128, 128)).T)
+    for c in range(slots // 128):
+        best = jnp.zeros((1, 128), jnp.int32)
+        for e in range(c + 1):
+            found = row_subs[e] == row_lanes[c]
+            if e == c:
+                found = found & (sub_slot < lane_slot)
+            best = jnp.maximum(best, jnp.max(jnp.where(found, sub_slot + (e * 128 + 1), 0), axis=0, keepdims=True))
+        prev_vec[:, pl.ds(c * 128, 128)] = best
+    for c in range(last_vec.shape[1] // 128):
+        best = jnp.zeros((1, 128), jnp.int32)
+        for e in range(slots // 128):
+            found = row_subs[e] == lane_slot + c * 128
+            best = jnp.maximum(best, jnp.max(jnp.where(found, sub_slot + (e * 128 + 1), 0), axis=0, keepdims=True))
+        last_vec[:, pl.ds(c * 128, 128)] = best
+    tables = [
+        pltpu.make_async_copy(prev_vec, prev_ref, load_sem.at[6]),
+        pltpu.make_async_copy(last_vec, last_ref, load_sem.at[7]),
+    ]
+    for copy in tables:
+        copy.start()
 
     arrive[0].wait_recv()
     forward_up = hop(4, down, 0, up)
     forward_up.start()
     over[2].start()
+    to_pair.wait_recv()
+    ring_start(0, mine[pl.ds(pl.multiple_of(k0 * load, 8), load)] + pair[...])
     arrive[2].wait_recv()
     forward_down = hop(5, up, 1, down)
     forward_down.start()
     over[5].start()
-    for i, j in ((1, 3), (3, 4), (4, 6), (5, 7)):
+    for i, j in ((1, 3), (3, 4)):
         arrive[i].wait_recv()
         over[j].start()
+    ring_start(1, ring_sum(0))
+    for i, j in ((4, 6), (5, 7)):
+        arrive[i].wait_recv()
+        over[j].start()
+    ring_start(2, ring_sum(1))
     for i, y in enumerate((y0, down, up, far)):
         for h in range(2):
             across(i * 2 + h, y, h, 1 - k0).wait_recv()
-    for copy in loads:
+    for copy in loads + tables:
         copy.wait()
 
     chain[0] = jnp.zeros((rhs, 128), F32)
@@ -148,9 +214,9 @@
 
     def products(i, _):
         base = i * step
-        made = [dot(xg[cols_ref[base + j]], tiles[base + j]) for j in range(step)]
+        made = [dot(xg[jnp.clip(cols_ref[0, 0, base + j], 0, 8 * seg_tiles - 1)], tiles[base + j]) for j in range(step)]
         for j in range(step):
-            chain[base + j + 1] = made[j] + chain[prev_ref[base + j]]
+            chain[base + j + 1] = made[j] + chain[prev_ref[0, base + j]]
         return 0
 
     lax.fori_loop(0, slots // step, products, 0)
@@ -166,7 +232,7 @@
 
     def partial(half, f, g, m):
         r = f * 4 + g if half == 0 else g * 4 + f
-        return chain[last_ref[r * seg_tiles + half * part + m]]
+        return chain[last_ref[0, r * seg_tiles + half * part + m]]
 
     def hop1(half, i):
         axis, pos = first[half]
@@ -202,6 +268,9 @@
         f0 = first[half][1]
         fill1(half, 2, near(f0, 1), 1)
         fill1(half, 3, near(f0, 3), 0)
+    whole[k0] = ring_sum(2) * F32(1.0 / total_rows)
+    back = send(whole.at[k0], whole.at[k0], ea_send.at[10], ea_recv.at[10], **{K: 1 - k0})
+    back.start()
     for half in range(2):
         f0 = first[half][1]
         hop1(half, 0).wait_recv()
@@ -221,6 +290,31 @@
     def over_part(body):
         lax.fori_loop(0, quarter, lambda m, _: (body(m), 0)[1], 0, unroll=8)
 
+    back.wait_recv()
+    products_of = jnp.concatenate([whole[0], whole[1]], axis=0)
+    basis_gram = products_of[:width]
+    guess = products_of[width:]
+    exact = lax.Precision.HIGHEST
+
+    def full(a, b, dims=(((1,), (0,)), ((), ()))):
+        return lax.dot_general(a, b, dims, precision=exact, preferred_element_type=F32)
+
+    guess_left = full(guess, basis_gram) - guess
+
+    def paired(a):
+        high, low = halves(a)
+        top = jnp.concatenate([high, high], axis=1)
+        return jnp.concatenate([top, jnp.concatenate([low, jnp.zeros_like(low)], axis=1)], axis=0)
+
+    guess_pair = paired(guess)
+
+    def lessen(i, _):
+        at = pl.ds(pl.multiple_of(i * CHUNK, CHUNK), CHUNK)
+        both = dot(guess_pair, q2[:, at])
+        w[:, at] = w[:, at] - (both[:rhs] + both[rhs:])
+        return 0
+
+    lax.fori_loop(0, seg // CHUNK, lessen, 0)
     for half in range(2):
         g0 = second[half][1]
         for i in range(2, 6):
@@ -276,65 +370,50 @@
 
         over_part(arrived_rows)
 
-    def total(value, use):
-        def inner_copy(d):
-            p = lax.rem(c0 + d, 8)
-            mine = inner.at[use, c0]
-            return send(
-                mine, mine, ar_send.at[use, d], ar_recv.at[use, d], **{Y: p // 2, K: lax.rem(p, 2)}
-            )
-
-        def outer_copy(d):
-            p = lax.rem(r0 + d, 16)
-            mine = outer.at[use, r0]
-            return send(
-                mine, mine, ar_send.at[use, 8 + d], ar_recv.at[use, 8 + d], **{X: p // 4, Z: lax.rem(p, 4)}
-            )
-
-        inner[use, c0] = value
-        for d in range(1, 8):
-            inner_copy(d).start()
-        for d in range(1, 8):
-            inner_copy(d).wait_recv()
-        acc = inner[use, 0]
-        for i in range(1, 8):
-            acc = acc + inner[use, i]
-        outer[use, r0] = acc
-        for d in range(1, 16):
-            outer_copy(d).start()
-        for d in range(1, 16):
-            outer_copy(d).wait_recv()
-        acc = outer[use, 0]
-        for i in range(1, 16):
-            acc = acc + outer[use, i]
-        for d in range(1, 8):
-            inner_copy(d).wait_send()
-        for d in range(1, 16):
-            outer_copy(d).wait_send()
-        return acc * F32(1.0 / total_rows)
+    def inner_copy(d):
+        p = lax.rem(c0 + d, 8)
+        ref = inner.at[c0]
+        return send(ref, ref, ar_send.at[d], ar_recv.at[d], **{Y: p // 2, K: lax.rem(p, 2)})
+
+    def outer_copy(d):
+        p = lax.rem(r0 + d, 16)
+        ref = outer.at[r0]
+        return send(ref, ref, ar_send.at[8 + d], ar_recv.at[8 + d], **{X: p // 4, Z: lax.rem(p, 4)})
 
     def project(i, acc):
         at = pl.ds(pl.multiple_of(i * CHUNK, CHUNK), CHUNK)
-        high, low = halves(w[:, at])
-        both = dot(jnp.concatenate([high, low], axis=0), qh[:, at], NT)
-        return acc + (both[:rhs] + both[rhs:] + dot(high, ql[:, at], NT))
-
-    coef = total(lax.fori_loop(0, seg // CHUNK, project, jnp.zeros((rhs, blocks * rhs), F32)), 0)
-    coef_ref[...] = coef
-    coef_high, coef_low = halves(coef)
-    coef_both = jnp.concatenate([coef_high, coef_low], axis=0)
-
-    def subtract(i, acc):
-        at = pl.ds(pl.multiple_of(i * CHUNK, CHUNK), CHUNK)
-        both = dot(coef_both, qh[:, at])
-        rest = w[:, at] - (both[:rhs] + both[rhs:] + dot(coef_high, ql[:, at]))
-        w[:, at] = rest
-        high, low = halves(rest)
-        both = dot(jnp.concatenate([high, low], axis=0), high, NT)
-        return acc + (both[:rhs] + both[rhs:] + dot(high, low, NT))
-
-    gram = lax.fori_loop(0, seg // CHUNK, subtract, jnp.zeros((rhs, rhs), F32))
-    gram = total(jnp.concatenate([gram, jnp.zeros((rhs, 128 - rhs), F32)], axis=1), 1)
+        stack = jnp.concatenate(halves(w[:, at]), axis=0)
+        return acc[0] + dot(stack, q2[:, at], NT), acc[1] + dot(stack, stack, NT)
+
+    with_basis, with_self = lax.fori_loop(
+        0, seg // CHUNK, project, (jnp.zeros((2 * rhs, 2 * width), F32), jnp.zeros((2 * rhs, 2 * rhs), F32))
+    )
+    inner[c0, pl.ds(0, rhs)] = with_basis[:rhs, :width] + with_basis[rhs:, :width] + with_basis[:rhs, width:]
+    with_self = with_self[:rhs, :rhs] + with_self[rhs:, :rhs] + with_self[:rhs, rhs:]
+    inner[c0, pl.ds(rhs, rhs)] = jnp.concatenate([with_self, jnp.zeros((rhs, 128 - rhs), F32)], axis=1)
+    for d in range(1, 8):
+        inner_copy(d).start()
+    for d in range(1, 8):
+        inner_copy(d).wait_recv()
+    acc = inner[0]
+    for i in range(1, 8):
+        acc = acc + inner[i]
+    outer[r0] = acc
+    for d in range(1, 16):
+        outer_copy(d).start()
+    for d in range(1, 16):
+        outer_copy(d).wait_recv()
+    acc = outer[0]
+    for i in range(1, 16):
+        acc = acc + outer[i]
+    acc = acc * F32(1.0 / total_rows)
+    reduced = acc[:rhs]
+    rest = reduced + guess_left
+    coef_ref[...] = rest + guess
+    basis_gram = jnp.concatenate([whole[0], whole[1]], axis=0)[:width]
+    turned = full(rest, basis_gram) - reduced
+    cross = full(turned, rest, NT) - full(rest, reduced, NT)
+    gram = acc[rhs:] + jnp.concatenate([cross, jnp.zeros((rhs, 128 - rhs), F32)], axis=1)
 
     row = lax.broadcasted_iota(jnp.int32, (rhs, 128), 0)
     lane = lax.broadcasted_iota(jnp.int32, (rhs, 128), 1)
@@ -345,14 +424,15 @@
     pivots = jnp.sum(jnp.where(lane == row, m, F32(0)), axis=1, keepdims=True)
     m = m / jnp.sqrt(pivots)
     tri_ref[...] = jnp.where(lane >= row, m, F32(0))[:, :rhs]
-    inv_high, inv_low = halves(m[:, rhs : 2 * rhs])
-    inv_both = jnp.concatenate([inv_high, inv_low], axis=0)
+    inverse = m[:, rhs : 2 * rhs]
+    back_pair = paired(-full(inverse, rest))
+    inverse_pair = paired(inverse)
 
     def solve(i, _):
         at = pl.ds(pl.multiple_of(i * CHUNK, CHUNK), CHUNK)
-        high, low = halves(w[:, at])
-        both = dot(inv_both, high)
-        out_ref[:, at] = both[:rhs] + both[rhs:] + dot(inv_high, low)
+        stack = jnp.concatenate(halves(w[:, at]), axis=0)
+        both = dot(back_pair, q2[:, at]) + dot(inverse_pair, stack)
+        out_ref[:, at] = both[:rhs] + both[rhs:]
         return 0
 
     lax.fori_loop(0, seg // CHUNK, solve, 0)
@@ -360,6 +440,21 @@
         for i in range(6):
             hop1(half, i).wait_send()
             hop2(half, i).wait_send()
+    for d in range(1, 8):
+        inner_copy(d).wait_send()
+    for d in range(1, 16):
+        outer_copy(d).wait_send()
+    to_pair.wait_send()
+    back.wait_send()
+    for i in range(3):
+        for d in range(1, 4):
+            ring_copy(i, d).wait_send()
+
+
+def finish(block_in, coef_in, triangle_in, block_out, coef_out, triangle_out):
+    block_out[...] = block_in[...]
+    coef_out[...] = coef_in[...].T
+    triangle_out[...] = triangle_in[...]
 
 
 def local(basis_blocks, tile_values, tile_rows, tile_column, tile_count, diagonal):
@@ -369,15 +464,6 @@
     part = seg_tiles // 2
     total_rows = seg * 128
     block_tiles = seg_tiles * 16
-
-    slot = jnp.arange(slots, dtype=jnp.int32)
-    live = slot < tile_count[0, 0]
-    rows = jnp.where(live, tile_rows[0, 0], -1)
-    cols = jnp.where(live, tile_column[0, 0], 0)
-    earlier = (rows[:, None] == rows[None, :]) & (slot[:, None] < slot[None, :])
-    prev = jnp.max(jnp.where(earlier, slot[:, None] + 1, 0), axis=0)
-    hit = rows[:, None] == jnp.arange(block_tiles, dtype=jnp.int32)[None, :]
-    last = jnp.max(jnp.where(hit, slot[:, None] + 1, 0), axis=0)
 
     smem = pl.BlockSpec(memory_space=pltpu.SMEM)
     vmem = pl.BlockSpec(memory_space=pltpu.VMEM)
@@ -391,15 +477,14 @@
             jax.ShapeDtypeStruct((rhs, blocks * rhs), F32),
             jax.ShapeDtypeStruct((rhs, rhs), F32),
         ),
-        in_specs=[smem, smem, smem, hbm, hbm, vmem],
+        in_specs=[smem, smem, vmem, hbm, hbm, vmem],
         out_specs=(vmem, vmem, vmem),
         scratch_shapes=[
             pltpu.VMEM((blocks, rhs, seg), F32),
             pltpu.VMEM((slots, 128, 128), BF16),
             pltpu.VMEM((8 * seg_tiles, *tile), BF16),
             pltpu.VMEM((slots + 8, *tile), F32),
-            pltpu.VMEM((blocks * rhs, seg), BF16),
-            pltpu.VMEM((blocks * rhs, seg), BF16),
+            pltpu.VMEM((2 * blocks * rhs, seg), BF16),
             pltpu.VMEM((rhs, seg), F32),
             pltpu.VMEM((2, 6, 2 * part, *tile), BF16),
             pltpu.VMEM((2, 6, 2 * part, *tile), BF16),
@@ -407,22 +492,43 @@
             pltpu.VMEM((2, 6, part // 2, *tile), BF16),
             pltpu.VMEM((2, 2, part // 2, *tile), F32),
             pltpu.VMEM((2, part, *tile), F32),
-            pltpu.VMEM((2, 8, *tile), F32),
-            pltpu.VMEM((2, 16, *tile), F32),
-            dma((6,)),
+            pltpu.VMEM((1, slots), jnp.int32),
+            pltpu.VMEM((1, block_tiles), jnp.int32),
+            pltpu.SMEM((1, slots), jnp.int32),
+            pltpu.SMEM((1, block_tiles), jnp.int32),
+            pltpu.VMEM((9 * rhs, 128), F32),
+            pltpu.VMEM((9 * rhs // 2, 128), F32),
+            pltpu.VMEM((3, 4, 9 * rhs // 2, 128), F32),
+            pltpu.VMEM((2, 9 * rhs // 2, 128), F32),
+            pltpu.VMEM((8, 2 * rhs, 128), F32),
+            pltpu.VMEM((16, 2 * rhs, 128), F32),
+            dma((8,)),
             dma((14,)),
             dma((14,)),
             dma((2, 12)),
             dma((2, 12)),
-            dma((2, 24)),
-            dma((2, 24)),
+            dma((11,)),
+            dma((11,)),
+            dma((24,)),
+            dma((24,)),
         ],
         compiler_params=pltpu.CompilerParams(
             collective_id=0, has_side_effects=True, vmem_limit_bytes=58 * 1024 * 1024
         ),
         name="step",
-    )(cols, prev, last, basis_blocks, tile_values[0, 0], diagonal[None, :])
-    return new_block, coef.T.reshape(blocks, rhs, rhs), triangle
+    )(tile_count, tile_column, tile_rows[0], basis_blocks, tile_values[0, 0], diagonal[None, :])
+    new_block, coef, triangle = pl.pallas_call(
+        finish,
+        out_shape=(
+            jax.ShapeDtypeStruct((rhs, seg), F32),
+            jax.ShapeDtypeStruct((blocks * rhs, rhs), F32),
+            jax.ShapeDtypeStruct((rhs, rhs), F32),
+        ),
+        in_specs=[vmem] * 3,
+        out_specs=(vmem,) * 3,
+        name="finish",
+    )(new_block, coef, triangle)
+    return new_block, coef.reshape(blocks, rhs, rhs), triangle
 
 
 def solution(mesh):

time: 91.7 us -> 76.5 us (0.83)
  Pallas kernels: 81.9 us -> 75 us
  local copies, waits for them, and re-layouts: 4.59 us -> 0 us
  other arithmetic: 3.63 us -> 0 us
    pallas_call x1, Pallas kernels: 81.9 us -> 73.1 us  [local(): pl.pallas_call(functools.partial(kernel, total_rows), out_shape=(jax.Shap...]
    unnamed x3 -> x0, local copies, waits for them, and re-layouts: 4.59 us -> none
    pallas_call x0 -> x1, Pallas kernels: none -> 1.9 us  [local(): pl.pallas_call(finish, out_shape=(jax.ShapeDtypeStruct((rhs, seg), F32),...]
    reduce_max x2 -> x0, other arithmetic: 1.64 us -> none  [the longest x1 0.88 us: local(): last = jnp.max(jnp.where(hit, slot[:, None] + 1, 0), axis=0)]
    unnamed x2 -> x0, other arithmetic: 1.4 us -> none
where the time goes in v2:
time: 76.5 us; the launch traced here: 76.3 us
  Pallas kernels  75 us (98%)
  between operations  1.29 us (2%)
    pallas_call x1, Pallas kernels, local(): pl.pallas_call(functools.partial(kernel, total_rows), out_shape=(jax.Shap...  73.1 us
    pallas_call x1, Pallas kernels, local(): pl.pallas_call(finish, out_shape=(jax.ShapeDtypeStruct((rhs, seg), F32),...  1.9 us

profile of v2, /device:TPU:1, one launch (start us, length us, event | category | flops | bytes accessed | tf_op | source)
XLA Modules:
  0.0 76.3 jit_solution(15301816961031530356)
XLA Ops:
  1.3 73.1 %step.1 = (f32[16,8192]{1,0:T(8,128)}, f32[16,128]{1,0:T(8,128)}, f32[16,16]{1,0:T(8,128)}) custom-call(s32[1,1]{1,0:T(1,128)S(6)} %copy.9.count_ref, s32[1,1,384]{2,1,0:T(1,128)} %cols_ref.1, s32[1,384]{1,0:T(1,128)} %bitcast.6, f32[8,16,8192]{2,1,0:T(8,128)} %basis_hbm.1, bf16[384,128,128]{2,1,0:T(8,128)(2,1)} %bitcast.4, f32[1,8192]{1,0:T(1,128)} %bitcast.5), custom_call_target="tpu_custom_call" | custom-call | tf_op jit(solution)/shard_map/step/pallas_call | solution.py:473
  74.4 1.9 %finish.1 = (f32[16,8192]{1,0:T(8,128)}, f32[128,16]{1,0:T(8,128)}, f32[16,16]{1,0:T(8,128)}) custom-call(f32[16,8192]{1,0:T(8,128)} %get-tuple-element.9.block_in, f32[16,128]{1,0:T(8,128)} %get-tuple-element.10.coef_in, f32[16,16]{1,0:T(8,128)} %get-tuple-element.11.triangle_in), custom_call_target="tpu_custom_call" | custom-call | tf_op jit(solution)/shard_map/finish/pallas_call | solution.py:520

commit v3 on v2

--- a/solution.py
+++ b/solution.py
@@ -41,7 +41,7 @@
     total_rows,
     count_ref, cols_ref, rows_ref, basis_hbm, tiles_hbm, diag_ref,
     out_ref, coef_ref, tri_ref,
-    basis, tiles, xg, chain, q2, w,
+    basis, tiles, xg, chain, q2, qt, w,
     sb1, rb1, sb2, rb2, zside, zown,
     prev_vec, last_vec, prev_ref, last_ref,
     mine, pair, ring, whole, inner, outer,
@@ -189,20 +189,16 @@
     forward_up = hop(4, down, 0, up)
     forward_up.start()
     over[2].start()
-    to_pair.wait_recv()
-    ring_start(0, mine[pl.ds(pl.multiple_of(k0 * load, 8), load)] + pair[...])
     arrive[2].wait_recv()
     forward_down = hop(5, up, 1, down)
     forward_down.start()
     over[5].start()
-    for i, j in ((1, 3), (3, 4)):
+    to_pair.wait_recv()
+    ring_start(0, mine[pl.ds(pl.multiple_of(k0 * load, 8), load)] + pair[...])
+    for i, j in ((1, 3), (3, 4), (4, 6), (5, 7)):
         arrive[i].wait_recv()
         over[j].start()
     ring_start(1, ring_sum(0))
-    for i, j in ((4, 6), (5, 7)):
-        arrive[i].wait_recv()
-        over[j].start()
-    ring_start(2, ring_sum(1))
     for i, y in enumerate((y0, down, up, far)):
         for h in range(2):
             across(i * 2 + h, y, h, 1 - k0).wait_recv()
@@ -210,7 +206,7 @@
         copy.wait()
 
     chain[0] = jnp.zeros((rhs, 128), F32)
-    step = 16
+    step = 48
 
     def products(i, _):
         base = i * step
@@ -221,6 +217,7 @@
 
     lax.fori_loop(0, slots // step, products, 0)
 
+    ring_start(2, ring_sum(1))
     for copy in hops + over + [forward_up, forward_down]:
         copy.wait_send()
 
@@ -315,6 +312,16 @@
         return 0
 
     lax.fori_loop(0, seg // CHUNK, lessen, 0)
+
+    def turn(i, _):
+        at = pl.ds(pl.multiple_of(i * 128, 128), 128)
+        flat = jnp.concatenate([basis[k, :, at] for k in range(blocks)], axis=0).T
+        high, low = halves(flat)
+        qt[at, pl.ds(0, width)] = high
+        qt[at, pl.ds(width, width)] = low
+        return 0
+
+    lax.fori_loop(0, seg_tiles, turn, 0, unroll=4)
     for half in range(2):
         g0 = second[half][1]
         for i in range(2, 6):
@@ -383,14 +390,15 @@
     def project(i, acc):
         at = pl.ds(pl.multiple_of(i * CHUNK, CHUNK), CHUNK)
         stack = jnp.concatenate(halves(w[:, at]), axis=0)
-        return acc[0] + dot(stack, q2[:, at], NT), acc[1] + dot(stack, stack, NT)
+        return acc[0] + dot(stack, qt[at, :]), acc[1] + dot(stack, stack, NT)
 
     with_basis, with_self = lax.fori_loop(
         0, seg // CHUNK, project, (jnp.zeros((2 * rhs, 2 * width), F32), jnp.zeros((2 * rhs, 2 * rhs), F32))
     )
     inner[c0, pl.ds(0, rhs)] = with_basis[:rhs, :width] + with_basis[rhs:, :width] + with_basis[:rhs, width:]
     with_self = with_self[:rhs, :rhs] + with_self[rhs:, :rhs] + with_self[:rhs, rhs:]
-    inner[c0, pl.ds(rhs, rhs)] = jnp.concatenate([with_self, jnp.zeros((rhs, 128 - rhs), F32)], axis=1)
+    folded = jnp.concatenate([with_self[:8], with_self[8:], jnp.zeros((8, 128 - 2 * rhs), F32)], axis=1)
+    inner[c0, pl.ds(rhs, 8)] = folded
     for d in range(1, 8):
         inner_copy(d).start()
     for d in range(1, 8):
@@ -409,11 +417,12 @@
     acc = acc * F32(1.0 / total_rows)
     reduced = acc[:rhs]
     rest = reduced + guess_left
-    coef_ref[...] = rest + guess
+    coef_ref[...] = (rest + guess).T
     basis_gram = jnp.concatenate([whole[0], whole[1]], axis=0)[:width]
     turned = full(rest, basis_gram) - reduced
     cross = full(turned, rest, NT) - full(rest, reduced, NT)
-    gram = acc[rhs:] + jnp.concatenate([cross, jnp.zeros((rhs, 128 - rhs), F32)], axis=1)
+    gram = jnp.concatenate([acc[rhs:, :rhs], acc[rhs:, rhs : 2 * rhs]], axis=0) + cross
+    gram = jnp.concatenate([gram, jnp.zeros((rhs, 128 - rhs), F32)], axis=1)
 
     row = lax.broadcasted_iota(jnp.int32, (rhs, 128), 0)
     lane = lax.broadcasted_iota(jnp.int32, (rhs, 128), 1)
@@ -451,12 +460,6 @@
             ring_copy(i, d).wait_send()
 
 
-def finish(block_in, coef_in, triangle_in, block_out, coef_out, triangle_out):
-    block_out[...] = block_in[...]
-    coef_out[...] = coef_in[...].T
-    triangle_out[...] = triangle_in[...]
-
-
 def local(basis_blocks, tile_values, tile_rows, tile_column, tile_count, diagonal):
     blocks, rhs, seg = basis_blocks.shape
     slots = tile_values.shape[2]
@@ -473,9 +476,9 @@
     new_block, coef, triangle = pl.pallas_call(
         functools.partial(kernel, total_rows),
         out_shape=(
-            jax.ShapeDtypeStruct((rhs, seg), F32),
-            jax.ShapeDtypeStruct((rhs, blocks * rhs), F32),
-            jax.ShapeDtypeStruct((rhs, rhs), F32),
+            pltpu.VMEM((rhs, seg), F32),
+            pltpu.VMEM((blocks * rhs, rhs), F32),
+            pltpu.VMEM((rhs, rhs), F32),
         ),
         in_specs=[smem, smem, vmem, hbm, hbm, vmem],
         out_specs=(vmem, vmem, vmem),
@@ -485,6 +488,7 @@
             pltpu.VMEM((8 * seg_tiles, *tile), BF16),
             pltpu.VMEM((slots + 8, *tile), F32),
             pltpu.VMEM((2 * blocks * rhs, seg), BF16),
+            pltpu.VMEM((seg, 2 * blocks * rhs), BF16),
             pltpu.VMEM((rhs, seg), F32),
             pltpu.VMEM((2, 6, 2 * part, *tile), BF16),
             pltpu.VMEM((2, 6, 2 * part, *tile), BF16),
@@ -500,8 +504,8 @@
             pltpu.VMEM((9 * rhs // 2, 128), F32),
             pltpu.VMEM((3, 4, 9 * rhs // 2, 128), F32),
             pltpu.VMEM((2, 9 * rhs // 2, 128), F32),
-            pltpu.VMEM((8, 2 * rhs, 128), F32),
-            pltpu.VMEM((16, 2 * rhs, 128), F32),
+            pltpu.VMEM((8, rhs + 8, 128), F32),
+            pltpu.VMEM((16, rhs + 8, 128), F32),
             dma((8,)),
             dma((14,)),
             dma((14,)),
@@ -517,17 +521,6 @@
         ),
         name="step",
     )(tile_count, tile_column, tile_rows[0], basis_blocks, tile_values[0, 0], diagonal[None, :])
-    new_block, coef, triangle = pl.pallas_call(
-        finish,
-        out_shape=(
-            jax.ShapeDtypeStruct((rhs, seg), F32),
-            jax.ShapeDtypeStruct((blocks * rhs, rhs), F32),
-            jax.ShapeDtypeStruct((rhs, rhs), F32),
-        ),
-        in_specs=[vmem] * 3,
-        out_specs=(vmem,) * 3,
-        name="finish",
-    )(new_block, coef, triangle)
     return new_block, coef.reshape(blocks, rhs, rhs), triangle
 
 

time: 76.5 us -> 72.2 us (0.944)
  Pallas kernels: 75 us -> 68.8 us
  local copies, waits for them, and re-layouts: 0 us -> 2.02 us
    pallas_call x2 -> x1, Pallas kernels: 75 us -> 68.8 us  [local(): pl.pallas_call(functools.partial(kernel, total_rows), out_shape=(pltpu.VM...]
    unnamed x0 -> x3, local copies, waits for them, and re-layouts: none -> 2.02 us
where the time goes in v3:
time: 72.2 us; the launch traced here: 72.1 us
  Pallas kernels  68.8 us (95%)
  local copies, waits for them, and re-layouts  2.02 us (3%)
  between operations  1.29 us (2%)
    pallas_call x1, Pallas kernels, local(): pl.pallas_call(functools.partial(kernel, total_rows), out_shape=(pltpu.VM...  68.8 us
    unnamed x3, local copies, waits for them, and re-layouts  2.02 us

profile of v3, /device:TPU:1, one launch (start us, length us, event | category | flops | bytes accessed | tf_op | source)
XLA Modules:
  0.0 72.1 jit_solution(17229205836723772872)
XLA Ops:
  1.3 68.8 %step.1 = (f32[16,8192]{1,0:T(8,128)S(1)}, f32[128,16]{1,0:T(8,128)S(1)}, f32[16,16]{1,0:T(8,128)S(1)}) custom-call(s32[1,1]{1,0:T(1,128)S(6)} %copy.15.count_ref, s32[1,1,384]{2,1,0:T(1,128)} %cols_ref.1, s32[1,384]{1,0:T(1,128)} %bitcast.7, f32[8,16,8192]{2,1,0:T(8,128)} %basis_hbm.1, bf16[384,128,128]{2,1,0:T(8,128)(2,1)} %bitcast.5, f32[1,8192]{1,0:T(1,128)} %bitcast.6), custom_call_target="tpu_custom_call" | custom-call | tf_op jit(solution)/shard_map/step/pallas_call | solution.py:476
  70.0 0.8 %copy.12 = f32[16,8192]{1,0:T(8,128)} copy(f32[16,8192]{1,0:T(8,128)S(1)} %get-tuple-element.9) | data formatting | bytes 1048576
  70.8 0.6 copy.13
  71.5 0.6 copy.14

commit v4 on v3

v4 whole, which is shorter than its diff:
```python
import functools

import jax
import jax.numpy as jnp
from jax import lax
from jax.experimental import pallas as pl
from jax.experimental.pallas import tpu as pltpu
from jax.sharding import Mesh
from jax.sharding import PartitionSpec as P

X, Z, Y, K = "row_0", "row_1", "col_0", "col_1"
ROW = (X, Z)
COL = (Y, K)
COL_ROW = (Y, K, X, Z)
MESH = pl.DeviceIdType.MESH
F32, BF16 = jnp.float32, jnp.bfloat16
NT = (((1,), (1,)), ((), ()))
CHUNK = 1024
LONG = 4096


def send(src, dst, send_sem, recv_sem, **to):
    return pltpu.make_async_remote_copy(
        src_ref=src, dst_ref=dst, send_sem=send_sem, recv_sem=recv_sem, device_id=to, device_id_type=MESH
    )


def halves(value):
    high = value.astype(BF16)
    return high, (value - high.astype(F32)).astype(BF16)


def dot(a, b, dims=(((1,), (0,)), ((), ()))):
    return lax.dot_general(a, b, dims, preferred_element_type=F32)


def lanes(m):
    return pl.ds(pl.multiple_of(m * 128, 128), 128)


def kernel(
    total_rows,
    count_hbm, cols_hbm, rows_hbm, basis_hbm, tiles_hbm, diag_hbm,
    out_ref, coef_ref, tri_ref,
    count_ref, cols_ref, rows_ref, diag_ref,
    basis, tiles, xg0, xg1, chain, q2, qt, w,
    sb1, rb1, sb2, rb2, zside,
    prev_vec, last_vec, prev_ref, last_ref,
    mine, pair, ring, whole, inner, outer,
    load_sem, ag_send, ag_recv, rs_send, rs_recv, ea_send, ea_recv, ar_send, ar_recv,
):
    x0, z0, y0, k0 = (lax.axis_index(a) for a in (X, Z, Y, K))
    blocks, rhs, seg = basis.shape
    slots = tiles.shape[0]
    seg_tiles = seg // 128
    part = seg_tiles // 2
    quarter = part // 2
    c0 = y0 * 2 + k0
    r0 = x0 * 4 + z0

    barrier = pltpu.get_barrier_semaphore()
    inner_peers = [lax.rem(c0 + d, 8) for d in range(1, 8)]
    outer_peers = [lax.rem(r0 + d, 16) for d in range(1, 16)]
    for p in inner_peers:
        pl.semaphore_signal(barrier, inc=1, device_id={Y: p // 2, K: lax.rem(p, 2)}, device_id_type=MESH)
    for p in outer_peers:
        pl.semaphore_signal(barrier, inc=1, device_id={X: p // 4, Z: lax.rem(p, 4)}, device_id_type=MESH)

    load_vector = pltpu.make_async_copy(basis_hbm.at[blocks - 1], basis.at[blocks - 1], load_sem.at[0])
    load_basis = pltpu.make_async_copy(
        basis_hbm.at[pl.ds(0, blocks - 1)], basis.at[pl.ds(0, blocks - 1)], load_sem.at[1]
    )
    load_vector.start()
    load_basis.start()
    piece = slots // 4
    loads = [
        pltpu.make_async_copy(
            tiles_hbm.at[pl.ds(i * piece, piece)], tiles.at[pl.ds(i * piece, piece)], load_sem.at[2 + i]
        )
        for i in range(4)
    ]
    small = [
        pltpu.make_async_copy(a, b, load_sem.at[8 + i])
        for i, (a, b) in enumerate(
            ((diag_hbm, diag_ref), (rows_hbm, rows_ref), (count_hbm, count_ref), (cols_hbm, cols_ref))
        )
    ]
    for copy in small + loads:
        copy.start()

    load_vector.wait()
    own = c0 * seg_tiles

    group = rhs // 2
    xg = (xg0, xg1)

    def to_tiles(q):
        def body(m, _):
            xg[q][own + m] = basis[blocks - 1, pl.ds(q * group, group), lanes(m)].astype(BF16)
            return 0

        lax.fori_loop(0, seg_tiles, body, 0, unroll=8)

    to_tiles(0)
    pl.semaphore_wait(barrier, 22)

    up, down, far = lax.rem(y0 + 1, 4), lax.rem(y0 + 3, 4), lax.rem(y0 + 2, 4)

    def chunk(q, y, k, h):
        return xg[q].at[pl.ds((y * 2 + k) * seg_tiles + h * part, part)]

    def hop(q, i, y, h, to):
        ref = chunk(q, y, k0, h)
        return send(ref, ref, ag_send.at[q, 0], ag_recv.at[q, i], **{Y: to})

    def across(q, y, h, k):
        ref = chunk(q, y, k, h)
        return send(ref, ref, ag_send.at[q, 1], ag_recv.at[q, 6], **{K: 1 - k0})

    hops = [
        [hop(q, 0, y0, 0, up), hop(q, 1, y0, 1, up), hop(q, 2, y0, 1, down), hop(q, 3, y0, 0, down)]
        for q in range(2)
    ]
    arrive = [
        [
            hop(q, 0, down, 0, up), hop(q, 1, down, 1, up), hop(q, 2, up, 1, down),
            hop(q, 3, up, 0, down), hop(q, 4, far, 0, up), hop(q, 5, far, 1, down),
        ]
        for q in range(2)
    ]
    forward = [[hop(q, 4, down, 0, up), hop(q, 5, up, 1, down)] for q in range(2)]
    places = list(enumerate((y0, down, up, far)))
    over = [[across(q, y, h, k0) for i, y in places for h in range(2)] for q in range(2)]

    def crossed(q):
        ref = xg[q].at[pl.ds(0, 4 * seg_tiles)]
        send(ref, ref, ag_send.at[q, 1], ag_recv.at[q, 6], **{K: 1 - k0}).wait_recv()

    def depart(q):
        for i in (0, 2, 1, 3):
            hops[q][i].start()
        over[q][0].start()
        over[q][1].start()

    def pass_on(q):
        for i, j, f in ((0, 2, 0), (2, 5, 1)):
            arrive[q][i].wait_recv()
            forward[q][f].start()
            over[q][j].start()

    def take(q, pairs):
        for i, j in pairs:
            arrive[q][i].wait_recv()
            over[q][j].start()

    depart(0)
    to_tiles(1)

    load_basis.wait()
    for copy in small:
        copy.wait()

    width = blocks * rhs

    def split_basis(i, acc):
        at = pl.ds(pl.multiple_of(i * CHUNK, CHUNK), CHUNK)
        for k in range(blocks):
            high, low = halves(basis[k, :, at])
            q2[pl.ds(k * rhs, rhs), at] = high
            q2[pl.ds(width + k * rhs, rhs), at] = low
        shifted = basis[blocks - 1, :, at] * diag_ref[:, at]
        w[:, at] = shifted
        stack = jnp.concatenate([q2[:, at], shifted.astype(BF16)], axis=0)
        return acc + dot(stack, q2[pl.ds(0, width), at], NT)

    made = lax.fori_loop(0, seg // CHUNK, split_basis, jnp.zeros((2 * width + rhs, width), F32))
    mine[pl.ds(0, width)] = made[:width] + made[width : 2 * width] + made[width : 2 * width].T
    mine[pl.ds(width, rhs)] = made[2 * width :]

    load = (width + rhs) // 2
    ring_axes = ((X, x0), (Z, z0), (Y, y0))
    to_pair = send(
        mine.at[pl.ds(pl.multiple_of((1 - k0) * load, 8), load)], pair, ea_send.at[0], ea_recv.at[0], **{K: 1 - k0}
    )
    to_pair.start()

    def ring_copy(i, d):
        axis, pos = ring_axes[i]
        ref = ring.at[i, pos]
        return send(ref, ref, ea_send.at[1], ea_recv.at[1 + i], **{axis: lax.rem(pos + d, 4)})

    def ring_start(i, value):
        ring[i, ring_axes[i][1]] = value
        for d in range(1, 4):
            ring_copy(i, d).start()

    def ring_sum(i):
        ref = ring.at[i, pl.ds(0, 3)]
        send(ref, ref, ea_send.at[1], ea_recv.at[1 + i], **{ring_axes[i][0]: 0}).wait_recv()
        return (ring[i, 0] + ring[i, 1]) + (ring[i, 2] + ring[i, 3])

    lane_slot = lax.broadcasted_iota(jnp.int32, (1, 128), 1)
    sub_slot = lax.broadcasted_iota(jnp.int32, (128, 128), 0)
    count = count_ref[...]
    row_lanes, row_subs = [], []
    for c in range(slots // 128):
        row_c = rows_ref[:, pl.ds(c * 128, 128)]
        row_c = jnp.where(lane_slot + c * 128 < count, row_c, -1)
        row_lanes.append(row_c)
        row_subs.append(jnp.broadcast_to(row_c, (128, 128)).T)
    for c in range(slots // 128):
        best = jnp.zeros((1, 128), jnp.int32)
        for e in range(c + 1):
            found = row_subs[e] == row_lanes[c]
            if e == c:
                found = found & (sub_slot < lane_slot)
            best = jnp.maximum(best, jnp.max(jnp.where(found, sub_slot + (e * 128 + 1), 0), axis=0, keepdims=True))
        prev_vec[:, pl.ds(c * 128, 128)] = best
    for c in range(last_vec.shape[1] // 128):
        best = jnp.zeros((1, 128), jnp.int32)
        for e in range(slots // 128):
            found = row_subs[e] == lane_slot + c * 128
            best = jnp.maximum(best, jnp.max(jnp.where(found, sub_slot + (e * 128 + 1), 0), axis=0, keepdims=True))
        last_vec[:, pl.ds(c * 128, 128)] = best
    tables = [
        pltpu.make_async_copy(prev_vec, prev_ref, load_sem.at[6]),
        pltpu.make_async_copy(last_vec, last_ref, load_sem.at[7]),
    ]
    for copy in tables:
        copy.start()

    pass_on(0)
    depart(1)
    to_pair.wait_recv()
    ring_start(0, mine[pl.ds(pl.multiple_of(k0 * load, 8), load)] + pair[...])
    take(0, ((1, 3), (3, 4), (4, 6), (5, 7)))
    crossed(0)
    for copy in loads + tables:
        copy.wait()

    step = 48
    trips = slots // step

    def products(q, start, stop):

        def body(i, _):
            base = i * step
            made = [
                dot(xg[q][jnp.clip(cols_ref[0, 0, base + j], 0, 8 * seg_tiles - 1)], tiles[base + j])
                for j in range(step)
            ]
            for j in range(step):
                chain[q, base + j + 1] = made[j] + chain[q, prev_ref[0, base + j]]
            return 0

        lax.fori_loop(start, stop, body, 0)

    chain[0, 0] = jnp.zeros((group, 128), F32)
    chain[1, 0] = jnp.zeros((group, 128), F32)
    products(0, 0, trips // 4)
    pass_on(1)
    take(1, ((1, 3), (3, 4)))
    products(0, trips // 4, trips // 2)
    ring_start(1, ring_sum(0))
    products(0, trips // 2, trips)
    take(1, ((4, 6), (5, 7)))

    first = ((X, x0), (Z, z0))
    second = ((Z, z0), (X, x0))

    def near(pos, d):
        return lax.rem(pos + d, 4)

    def partial(q, half, f, g, p):
        r = f * 4 + g if half == 0 else g * 4 + f
        at = r * seg_tiles + half * part + 2 * p
        return jnp.concatenate([chain[q, last_ref[0, at]], chain[q, last_ref[0, at + 1]]], axis=0)

    ahead = (2, 1, 3, 0)
    eighth = quarter // 2
    onward, stay = (0, 1, 2), (3,)

    def hop1(q, half, i, os):
        axis, pos = first[half]
        n = 2 * q + half
        at = pl.ds(os[0] * eighth, len(os) * eighth)
        return send(
            sb1.at[n, i, at], rb1.at[n, i, at], rs_send.at[0], rs_recv.at[n, min(i, 2) + (3 if os == stay else 0)],
            **{axis: near(pos, 1 if i % 2 == 0 else 3)},
        )

    def hop2(q, half, i):
        axis, pos = second[half]
        n = 2 * q + half
        return send(
            sb2.at[n, i], rb2.at[n, i], rs_send.at[1], rs_recv.at[n, 6 + min(i, 2)],
            **{axis: near(pos, 1 if i % 2 == 0 else 3)},
        )

    def own_block(q, half, f, o, p):
        return partial(q, half, f, near(second[half][1], ahead[o]), p)

    def fill1(q, half, i, f, h, os, arrived=None):
        n = 2 * q + half

        def body(p, _):
            for o in os:
                value = own_block(q, half, f, o, h * eighth + p)
                if arrived is not None:
                    value = value + rb1[n, arrived, o * eighth + p].astype(F32)
                sb1[n, i, o * eighth + p] = value.astype(BF16)
            return 0

        lax.fori_loop(0, eighth, body, 0, unroll=8)
        hop1(q, half, i, os).start()

    def phase1(q, os):
        for half in range(2):
            f0 = first[half][1]
            fill1(q, half, 0, near(f0, 2), 0, os)
            fill1(q, half, 1, near(f0, 2), 1, os)
        for half in range(2):
            f0 = first[half][1]
            fill1(q, half, 2, near(f0, 1), 1, os)
            fill1(q, half, 3, near(f0, 3), 0, os)

    def phase1_rest(q, os):
        for half in range(2):
            f0 = first[half][1]
            hop1(q, half, 0, os).wait_recv()
            fill1(q, half, 4, near(f0, 1), 0, os, 0)
            hop1(q, half, 1, os).wait_recv()
            fill1(q, half, 5, near(f0, 3), 1, os, 1)

    def wait_rest1(q, half, os):
        n = 2 * q + half
        ref = rb1.at[n, pl.ds(2, 4), pl.ds(os[0] * eighth, len(os) * eighth)]
        send(ref, ref, rs_send.at[0], rs_recv.at[n, 2 + (3 if os == stay else 0)], **{X: 0}).wait_recv()

    def wait_rest2(q, half):
        n = 2 * q + half
        ref = rb2.at[n, pl.ds(2, 4)]
        send(ref, ref, rs_send.at[1], rs_recv.at[n, 8], **{X: 0}).wait_recv()

    def summed1(q, half, o, h, p):
        n = 2 * q + half
        return (
            own_block(q, half, first[half][1], o, h * eighth + p)
            + rb1[n, 3 - h, o * eighth + p].astype(F32)
            + rb1[n, 4 + h, o * eighth + p].astype(F32)
        )

    def over_part(body):
        lax.fori_loop(0, eighth, lambda p, _: (body(p), 0)[1], 0, unroll=8)

    def phase2(q):
        for half in range(2):
            n = 2 * q + half
            wait_rest1(q, half, onward)

            def far_block(p):
                sb2[n, 0, p] = summed1(q, half, 0, 0, p).astype(BF16)
                sb2[n, 1, p] = summed1(q, half, 0, 1, p).astype(BF16)

            over_part(far_block)
            hop2(q, half, 0).start()
            hop2(q, half, 1).start()
        for half in range(2):
            n = 2 * q + half

            def near_block(p):
                sb2[n, 2, p] = summed1(q, half, 1, 1, p).astype(BF16)
                sb2[n, 3, p] = summed1(q, half, 2, 0, p).astype(BF16)

            over_part(near_block)
            hop2(q, half, 2).start()
            hop2(q, half, 3).start()
        for half in range(2):
            n = 2 * q + half

            def kept(p):
                zside[n, 0, p] = summed1(q, half, 1, 0, p)
                zside[n, 1, p] = summed1(q, half, 2, 1, p)

            over_part(kept)

    def phase2_rest(q):
        for half in range(2):
            n = 2 * q + half
            hop2(q, half, 0).wait_recv()
            hop2(q, half, 1).wait_recv()

            def joined(p):
                sb2[n, 4, p] = (zside[n, 0, p] + rb2[n, 0, p].astype(F32)).astype(BF16)
                sb2[n, 5, p] = (zside[n, 1, p] + rb2[n, 1, p].astype(F32)).astype(BF16)

            over_part(joined)
            hop2(q, half, 4).start()
            hop2(q, half, 5).start()

    def place(q, half, m, value):
        for e in range(2):
            at = (pl.ds(q * group, group), lanes(half * part + m + e))
            w[at] = w[at] + value[e * group : (e + 1) * group]

    def stayed(q):
        for half in range(2):
            wait_rest1(q, half, stay)

            def body(p):
                place(q, half, 2 * p, summed1(q, half, 3, 0, p))
                place(q, half, quarter + 2 * p, summed1(q, half, 3, 1, p))

            over_part(body)

    def landed(q):
        for half in range(2):
            n = 2 * q + half
            wait_rest2(q, half)

            def body(p):
                place(q, half, 2 * p, rb2[n, 3, p].astype(F32) + rb2[n, 4, p].astype(F32))
                place(q, half, quarter + 2 * p, rb2[n, 2, p].astype(F32) + rb2[n, 5, p].astype(F32))

            over_part(body)

    phase1(0, onward)
    phase1(0, stay)
    crossed(1)
    products(1, 0, trips // 2)
    ring_start(2, ring_sum(1))
    products(1, trips // 2, trips)
    phase1_rest(0, onward)
    phase1(1, onward)
    phase1_rest(0, stay)
    phase1(1, stay)
    whole[k0] = ring_sum(2) * F32(1.0 / total_rows)
    back = send(whole.at[k0], whole.at[k0], ea_send.at[2], ea_recv.at[4], **{K: 1 - k0})
    back.start()
    for q in range(2):
        ref = xg[q].at[pl.ds(0, 3 * seg_tiles)]
        send(ref, ref, ag_send.at[q, 0], ag_recv.at[q, 0], **{Y: up}).wait_send()
        ref = xg[q].at[pl.ds(0, 4 * seg_tiles)]
        send(ref, ref, ag_send.at[q, 1], ag_recv.at[q, 6], **{K: 1 - k0}).wait_send()
    back.wait_recv()
    products_of = jnp.concatenate([whole[0], whole[1]], axis=0)
    basis_gram = products_of[:width]
    guess = products_of[width:]
    exact = lax.Precision.HIGHEST

    def full(a, b, dims=(((1,), (0,)), ((), ()))):
        return lax.dot_general(a, b, dims, precision=exact, preferred_element_type=F32)

    guess_left = full(guess, basis_gram) - guess

    def paired(a):
        high, low = halves(a)
        top = jnp.concatenate([high, high], axis=1)
        return jnp.concatenate([top, jnp.concatenate([low, jnp.zeros_like(low)], axis=1)], axis=0)

    guess_pair = paired(guess)

    def lessen(i, _):
        at = pl.ds(pl.multiple_of(i * CHUNK, CHUNK), CHUNK)
        both = dot(guess_pair, q2[:, at])
        w[:, at] = w[:, at] - (both[:rhs] + both[rhs:])
        return 0

    lax.fori_loop(0, seg // CHUNK, lessen, 0)
    phase2(0)

    def turn(i, _):
        at = pl.ds(pl.multiple_of(i * 128, 128), 128)
        flat = jnp.concatenate([basis[k, :, at] for k in range(blocks)], axis=0).T
        high, low = halves(flat)
        qt[at, pl.ds(0, width)] = high
        qt[at, pl.ds(width, width)] = low
        return 0

    lax.fori_loop(0, seg_tiles, turn, 0, unroll=4)
    phase1_rest(1, onward)
    phase2(1)
    phase2_rest(0)
    phase1_rest(1, stay)
    stayed(0)
    phase2_rest(1)
    landed(0)
    stayed(1)
    landed(1)

    def inner_copy(d):
        p = lax.rem(c0 + d, 8)
        ref = inner.at[c0]
        return send(ref, ref, ar_send.at[0], ar_recv.at[0], **{Y: p // 2, K: lax.rem(p, 2)})

    def outer_copy(d):
        p = lax.rem(r0 + d, 16)
        ref = outer.at[r0]
        return send(ref, ref, ar_send.at[1], ar_recv.at[1], **{X: p // 4, Z: lax.rem(p, 4)})

    def inner_all():
        ref = inner.at[pl.ds(0, 7)]
        return send(ref, ref, ar_send.at[0], ar_recv.at[0], **{Y: 0})

    def outer_all():
        ref = outer.at[pl.ds(0, 15)]
        return send(ref, ref, ar_send.at[1], ar_recv.at[1], **{X: 0})

    def project(i, acc):
        at = pl.ds(pl.multiple_of(i * LONG, LONG), LONG)
        stack = jnp.concatenate(halves(w[:, at]), axis=0)
        return acc[0] + dot(stack, qt[at, :]), acc[1] + dot(stack, stack, NT)

    with_basis, with_self = lax.fori_loop(
        0, seg // LONG, project, (jnp.zeros((2 * rhs, 2 * width), F32), jnp.zeros((2 * rhs, 2 * rhs), F32))
    )
    inner[c0, pl.ds(0, rhs)] = with_basis[:rhs, :width] + with_basis[rhs:, :width] + with_basis[:rhs, width:]
    with_self = with_self[:rhs, :rhs] + with_self[rhs:, :rhs] + with_self[:rhs, rhs:]
    folded = jnp.concatenate([with_self[:8], with_self[8:], jnp.zeros((8, 128 - 2 * rhs), F32)], axis=1)
    inner[c0, pl.ds(rhs, 8)] = folded
    for d in range(1, 8):
        inner_copy(d).start()
    inner_all().wait_recv()
    acc = inner[0]
    for i in range(1, 8):
        acc = acc + inner[i]
    outer[r0] = acc
    for d in range(1, 16):
        outer_copy(d).start()
    outer_all().wait_recv()
    acc = outer[0]
    for i in range(1, 16):
        acc = acc + outer[i]
    acc = acc * F32(1.0 / total_rows)
    reduced = acc[:rhs]
    rest = reduced + guess_left
    coef_ref[...] = (rest + guess).T
    basis_gram = jnp.concatenate([whole[0], whole[1]], axis=0)[:width]
    turned = full(rest, basis_gram) - reduced
    cross = full(turned, rest, NT) - full(rest, reduced, NT)
    gram = jnp.concatenate([acc[rhs:, :rhs], acc[rhs:, rhs : 2 * rhs]], axis=0) + cross
    gram = jnp.concatenate([gram, jnp.zeros((rhs, 128 - rhs), F32)], axis=1)

    row = lax.broadcasted_iota(jnp.int32, (rhs, 128), 0)
    lane = lax.broadcasted_iota(jnp.int32, (rhs, 128), 1)
    m = jnp.where(lane < rhs, gram, jnp.where(lane - rhs == row, F32(1), F32(0)))
    for k in range(rhs - 1):
        column = jnp.broadcast_to(m[:, k : k + 1], m.shape)
        m = m - jnp.where(row > k, column * (1.0 / column[k : k + 1, :]), F32(0)) * m[k : k + 1, :]
    pivots = jnp.sum(jnp.where(lane == row, m, F32(0)), axis=1, keepdims=True)
    m = m / jnp.sqrt(pivots)
    tri_ref[...] = jnp.where(lane >= row, m, F32(0))[:, :rhs]
    inverse = m[:, rhs : 2 * rhs]
    back_pair = paired(-full(inverse, rest))
    inverse_pair = paired(inverse)

    def solve(i, _):
        at = pl.ds(pl.multiple_of(i * LONG, LONG), LONG)
        stack = jnp.concatenate(halves(w[:, at]), axis=0)
        both = dot(back_pair, q2[:, at]) + dot(inverse_pair, stack)
        out_ref[:, at] = both[:rhs] + both[rhs:]
        return 0

    lax.fori_loop(0, seg // LONG, solve, 0)
    send(sb1, sb1, rs_send.at[0], rs_recv.at[0, 0], **{X: 0}).wait_send()
    send(sb2, sb2, rs_send.at[1], rs_recv.at[0, 0], **{X: 0}).wait_send()
    inner_all().wait_send()
    outer_all().wait_send()
    to_pair.wait_send()
    back.wait_send()
    ref = ring.at[:, pl.ds(0, 3)]
    send(ref, ref, ea_send.at[1], ea_recv.at[1], **{X: 0}).wait_send()


def local(basis_blocks, tile_values, tile_rows, tile_column, tile_count, diagonal):
    blocks, rhs, seg = basis_blocks.shape
    slots = tile_values.shape[2]
    seg_tiles = seg // 128
    part = seg_tiles // 2
    total_rows = seg * 128
    block_tiles = seg_tiles * 16

    vmem = pl.BlockSpec(memory_space=pltpu.VMEM)
    hbm = pl.BlockSpec(memory_space=pl.ANY)
    dma = pltpu.SemaphoreType.DMA
    tile = (rhs, 128)
    new_block, coef, triangle = pl.pallas_call(
        functools.partial(kernel, total_rows),
        out_shape=(
            pltpu.VMEM((rhs, seg), F32),
            pltpu.VMEM((blocks * rhs, rhs), F32),
            pltpu.VMEM((rhs, rhs), F32),
        ),
        in_specs=[hbm] * 6,
        out_specs=(vmem, vmem, vmem),
        scratch_shapes=[
            pltpu.VMEM((1, 1), jnp.int32),
            pltpu.SMEM((1, 1, slots), jnp.int32),
            pltpu.VMEM((1, slots), jnp.int32),
            pltpu.VMEM((1, seg), F32),
            pltpu.VMEM((blocks, rhs, seg), F32),
            pltpu.VMEM((slots, 128, 128), BF16),
            pltpu.VMEM((8 * seg_tiles, rhs // 2, 128), BF16),
            pltpu.VMEM((8 * seg_tiles, rhs // 2, 128), BF16),
            pltpu.VMEM((2, slots + 8, rhs // 2, 128), F32),
            pltpu.VMEM((2 * blocks * rhs, seg), BF16),
            pltpu.VMEM((seg, 2 * blocks * rhs), BF16),
            pltpu.VMEM((rhs, seg), F32),
            pltpu.VMEM((4, 6, part, *tile), BF16),
            pltpu.VMEM((4, 6, part, *tile), BF16),
            pltpu.VMEM((4, 6, part // 4, *tile), BF16),
            pltpu.VMEM((4, 6, part // 4, *tile), BF16),
            pltpu.VMEM((4, 2, part // 4, *tile), F32),
            pltpu.VMEM((1, slots), jnp.int32),
            pltpu.VMEM((1, block_tiles), jnp.int32),
            pltpu.SMEM((1, slots), jnp.int32),
            pltpu.SMEM((1, block_tiles), jnp.int32),
            pltpu.VMEM((9 * rhs, 128), F32),
            pltpu.VMEM((9 * rhs // 2, 128), F32),
            pltpu.VMEM((3, 4, 9 * rhs // 2, 128), F32),
            pltpu.VMEM((2, 9 * rhs // 2, 128), F32),
            pltpu.VMEM((8, rhs + 8, 128), F32),
            pltpu.VMEM((16, rhs + 8, 128), F32),
            dma((12,)),
            dma((2, 2)),
            dma((2, 7)),
            dma((2,)),
            dma((4, 9)),
            dma((3,)),
            dma((5,)),
            dma((2,)),
            dma((2,)),
        ],
        compiler_params=pltpu.CompilerParams(
            collective_id=0, has_side_effects=True, vmem_limit_bytes=58 * 1024 * 1024
        ),
        name="step",
    )(tile_count, tile_column, tile_rows[0], basis_blocks, tile_values[0, 0], diagonal[None, :])
    return new_block, coef.reshape(blocks, rhs, rhs), triangle


def solution(mesh):
    split = Mesh(mesh.devices.reshape(4, 4, 4, 2), (X, Z, Y, K))
    placed = (
        P(None, None, COL_ROW),
        P(COL, ROW, None, None, None),
        P(COL, ROW, None),
        P(COL, ROW, None),
        P(COL, ROW),
        P(COL_ROW),
    )
    return jax.shard_map(
        local, mesh=split, in_specs=placed, out_specs=(P(None, COL_ROW), P(), P()), check_vma=False
    )
```

time: 72.2 us -> 66.8 us (0.925)
  Pallas kernels: 68.8 us -> 63.3 us
    pallas_call x1, Pallas kernels: 68.8 us -> 63.3 us  [local(): pl.pallas_call(functools.partial(kernel, total_rows), out_shape=(pltpu.VM...]
where the time goes in v4:
time: 66.8 us; the launch traced here: 66.6 us
  Pallas kernels  63.3 us (95%)
  local copies, waits for them, and re-layouts  2.02 us (3%)
  between operations  1.29 us (2%)
    pallas_call x1, Pallas kernels, local(): pl.pallas_call(functools.partial(kernel, total_rows), out_shape=(pltpu.VM...  63.3 us
    unnamed x3, local copies, waits for them, and re-layouts  2.02 us

profile of v4, /device:TPU:1, one launch (start us, length us, event | category | flops | bytes accessed | tf_op | source)
XLA Modules:
  0.0 66.6 jit_solution(12532689170340593260)
XLA Ops:
  1.3 63.3 %step.1 = (f32[16,8192]{1,0:T(8,128)S(1)}, f32[128,16]{1,0:T(8,128)S(1)}, f32[16,16]{1,0:T(8,128)S(1)}) custom-call(s32[1,1]{1,0:T(1,128)S(6)} %copy.15.count_hbm, s32[1,1,384]{2,1,0:T(1,128)} %cols_hbm.1, s32[1,384]{1,0:T(1,128)} %bitcast.7, f32[8,16,8192]{2,1,0:T(8,128)} %basis_hbm.1, bf16[384,128,128]{2,1,0:T(8,128)(2,1)} %bitcast.5, f32[1,8192]{1,0:T(1,128)} %bitcast.6), custom_call_target="tpu_custom_call" | custom-call | tf_op jit(solution)/shard_map/step/pallas_call | solution.py:587
  64.6 0.8 %copy.12 = f32[16,8192]{1,0:T(8,128)} copy(f32[16,8192]{1,0:T(8,128)S(1)} %get-tuple-element.9) | data formatting | bytes 1048576
  65.4 0.6 copy.13
  66.0 0.6 copy.14

commit v5 on v4

--- a/solution.py
+++ b/solution.py
@@ -17,6 +17,7 @@
 NT = (((1,), (1,)), ((), ()))
 CHUNK = 1024
 LONG = 4096
+FINISH = 2048
 
 
 def send(src, dst, send_sem, recv_sem, **to):
@@ -41,9 +42,9 @@
 def kernel(
     total_rows,
     count_hbm, cols_hbm, rows_hbm, basis_hbm, tiles_hbm, diag_hbm,
-    out_ref, coef_ref, tri_ref,
+    w, q2, pairs_ref, coef_ref, tri_ref,
     count_ref, cols_ref, rows_ref, diag_ref,
-    basis, tiles, xg0, xg1, chain, q2, qt, w,
+    basis, tiles, xg0, xg1, chain, qt,
     sb1, rb1, sb2, rb2, zside,
     prev_vec, last_vec, prev_ref, last_ref,
     mine, pair, ring, whole, inner, outer,
@@ -433,7 +434,6 @@
     phase1_rest(0, onward)
     phase1(1, onward)
     phase1_rest(0, stay)
-    phase1(1, stay)
     whole[k0] = ring_sum(2) * F32(1.0 / total_rows)
     back = send(whole.at[k0], whole.at[k0], ea_send.at[2], ea_recv.at[4], **{K: 1 - k0})
     back.start()
@@ -467,7 +467,9 @@
         return 0
 
     lax.fori_loop(0, seg // CHUNK, lessen, 0)
+    phase1_rest(1, onward)
     phase2(0)
+    phase1(1, stay)
 
     def turn(i, _):
         at = pl.ds(pl.multiple_of(i * 128, 128), 128)
@@ -478,7 +480,6 @@
         return 0
 
     lax.fori_loop(0, seg_tiles, turn, 0, unroll=4)
-    phase1_rest(1, onward)
     phase2(1)
     phase2_rest(0)
     phase1_rest(1, stay)
@@ -551,17 +552,10 @@
     m = m / jnp.sqrt(pivots)
     tri_ref[...] = jnp.where(lane >= row, m, F32(0))[:, :rhs]
     inverse = m[:, rhs : 2 * rhs]
-    back_pair = paired(-full(inverse, rest))
-    inverse_pair = paired(inverse)
-
-    def solve(i, _):
-        at = pl.ds(pl.multiple_of(i * LONG, LONG), LONG)
-        stack = jnp.concatenate(halves(w[:, at]), axis=0)
-        both = dot(back_pair, q2[:, at]) + dot(inverse_pair, stack)
-        out_ref[:, at] = both[:rhs] + both[rhs:]
-        return 0
-
-    lax.fori_loop(0, seg // LONG, solve, 0)
+    pairs_ref[:, pl.ds(0, 2 * width)] = paired(-full(inverse, rest))
+    pairs_ref[:, pl.ds(2 * width, 128)] = jnp.concatenate(
+        [paired(inverse), jnp.zeros((2 * rhs, 128 - 2 * rhs), BF16)], axis=1
+    )
     send(sb1, sb1, rs_send.at[0], rs_recv.at[0, 0], **{X: 0}).wait_send()
     send(sb2, sb2, rs_send.at[1], rs_recv.at[0, 0], **{X: 0}).wait_send()
     inner_all().wait_send()
@@ -572,6 +566,27 @@
     send(ref, ref, ea_send.at[1], ea_recv.at[1], **{X: 0}).wait_send()
 
 
+def finish(w, q2, pairs, coef, tri, out_hbm, coef_hbm, tri_hbm, made, sem):
+    rhs, seg = w.shape
+    deep = q2.shape[0]
+    count = seg // FINISH
+    copies = [
+        pltpu.make_async_copy(coef, coef_hbm, sem.at[count]),
+        pltpu.make_async_copy(tri, tri_hbm, sem.at[count + 1]),
+    ]
+    for copy in copies:
+        copy.start()
+    for i in range(count):
+        at = pl.ds(i * FINISH, FINISH)
+        stack = jnp.concatenate(halves(w[:, at]), axis=0)
+        both = dot(pairs[:, :deep], q2[:, at]) + dot(pairs[:, deep : deep + 2 * rhs], stack)
+        made[:, at] = both[:rhs] + both[rhs:]
+        copies.append(pltpu.make_async_copy(made.at[:, at], out_hbm.at[:, at], sem.at[i]))
+        copies[-1].start()
+    for copy in copies:
+        copy.wait()
+
+
 def local(basis_blocks, tile_values, tile_rows, tile_column, tile_count, diagonal):
     blocks, rhs, seg = basis_blocks.shape
     slots = tile_values.shape[2]
@@ -584,15 +599,17 @@
     hbm = pl.BlockSpec(memory_space=pl.ANY)
     dma = pltpu.SemaphoreType.DMA
     tile = (rhs, 128)
-    new_block, coef, triangle = pl.pallas_call(
+    held = pl.pallas_call(
         functools.partial(kernel, total_rows),
         out_shape=(
             pltpu.VMEM((rhs, seg), F32),
+            pltpu.VMEM((2 * blocks * rhs, seg), BF16),
+            pltpu.VMEM((2 * rhs, 2 * blocks * rhs + 128), BF16),
             pltpu.VMEM((blocks * rhs, rhs), F32),
             pltpu.VMEM((rhs, rhs), F32),
         ),
         in_specs=[hbm] * 6,
-        out_specs=(vmem, vmem, vmem),
+        out_specs=(vmem,) * 5,
         scratch_shapes=[
             pltpu.VMEM((1, 1), jnp.int32),
             pltpu.SMEM((1, 1, slots), jnp.int32),
@@ -603,9 +620,7 @@
             pltpu.VMEM((8 * seg_tiles, rhs // 2, 128), BF16),
             pltpu.VMEM((8 * seg_tiles, rhs // 2, 128), BF16),
             pltpu.VMEM((2, slots + 8, rhs // 2, 128), F32),
-            pltpu.VMEM((2 * blocks * rhs, seg), BF16),
             pltpu.VMEM((seg, 2 * blocks * rhs), BF16),
-            pltpu.VMEM((rhs, seg), F32),
             pltpu.VMEM((4, 6, part, *tile), BF16),
             pltpu.VMEM((4, 6, part, *tile), BF16),
             pltpu.VMEM((4, 6, part // 4, *tile), BF16),
@@ -632,10 +647,23 @@
             dma((2,)),
         ],
         compiler_params=pltpu.CompilerParams(
-            collective_id=0, has_side_effects=True, vmem_limit_bytes=58 * 1024 * 1024
+            collective_id=0, has_side_effects=True, vmem_limit_bytes=50 * 1024 * 1024
         ),
         name="step",
     )(tile_count, tile_column, tile_rows[0], basis_blocks, tile_values[0, 0], diagonal[None, :])
+    new_block, coef, triangle = pl.pallas_call(
+        finish,
+        out_shape=(
+            jax.ShapeDtypeStruct((rhs, seg), F32),
+            jax.ShapeDtypeStruct((blocks * rhs, rhs), F32),
+            jax.ShapeDtypeStruct((rhs, rhs), F32),
+        ),
+        in_specs=[vmem] * 5,
+        out_specs=(hbm,) * 3,
+        scratch_shapes=[pltpu.VMEM((rhs, seg), F32), dma((seg // FINISH + 2,))],
+        compiler_params=pltpu.CompilerParams(vmem_limit_bytes=4 * 1024 * 1024),
+        name="finish",
+    )(*[pltpu.with_memory_space_constraint(a, pltpu.VMEM) for a in held])
     return new_block, coef.reshape(blocks, rhs, rhs), triangle
 
 

time: 66.8 us -> 63.2 us (0.946)
  local copies, waits for them, and re-layouts: 2.02 us -> 0 us
  Pallas kernels: 63.3 us -> 61.8 us
    pallas_call x1, Pallas kernels: 63.3 us -> 60.1 us  [local(): pl.pallas_call(functools.partial(kernel, total_rows), out_shape=(pltpu.VM...]
    unnamed x3 -> x0, local copies, waits for them, and re-layouts: 2.02 us -> none
    pallas_call x0 -> x1, Pallas kernels: none -> 1.72 us  [local(): pl.pallas_call(finish, out_shape=(jax.ShapeDtypeStruct((rhs, seg), F32),...]
where the time goes in v5:
time: 63.2 us; the launch traced here: 63.1 us
  Pallas kernels  61.8 us (98%)
  between operations  1.29 us (2%)
    pallas_call x1, Pallas kernels, local(): pl.pallas_call(functools.partial(kernel, total_rows), out_shape=(pltpu.VM...  60.1 us
    pallas_call x1, Pallas kernels, local(): pl.pallas_call(finish, out_shape=(jax.ShapeDtypeStruct((rhs, seg), F32),...  1.72 us

profile of v5, /device:TPU:1, one launch (start us, length us, event | category | flops | bytes accessed | tf_op | source)
XLA Modules:
  0.0 63.1 jit_solution(18301025960348124197)
XLA Ops:
  1.3 60.1 %step.1 = (f32[16,8192]{1,0:T(8,128)S(1)}, bf16[256,8192]{1,0:T(8,128)(2,1)S(1)}, bf16[32,384]{1,0:T(8,128)(2,1)S(1)}, f32[128,16]{1,0:T(8,128)S(1)}, f32[16,16]{1,0:T(8,128)S(1)}) custom-call(s32[1,1]{1,0:T(1,128)S(6)} %copy.9.count_hbm, s32[1,1,384]{2,1,0:T(1,128)} %cols_hbm.1, s32[1,384]{1,0:T(1,128)} %bitcast.6, f32[8,16,8192]{2,1,0:T(8,128)} %basis_hbm.1, ...), custom_call_target="tpu_custom_call" | custom-call | tf_op jit(solution)/shard_map/step/pallas_call | solution.py:602
  61.4 1.7 %finish.1 = (f32[16,8192]{1,0:T(8,128)}, f32[128,16]{1,0:T(8,128)}, f32[16,16]{1,0:T(8,128)}) custom-call(f32[16,8192]{1,0:T(8,128)S(1)} %get-tuple-element.11.w, bf16[256,8192]{1,0:T(8,128)(2,1)S(1)} %get-tuple-element.12.q2, bf16[32,384]{1,0:T(8,128)(2,1)S(1)} %get-tuple-element.13.pairs, f32[128,16]{1,0:T(8,128)S(1)} %get-tuple-element.14.coef, ...), custom_call_target="tpu_custom_call" | custom-call | tf_op jit(solution)/shard_map/finish/pallas_call | solution.py:654

commit v6 on v5

--- a/solution.py
+++ b/solution.py
@@ -239,7 +239,7 @@
     for copy in loads + tables:
         copy.wait()
 
-    step = 48
+    step = 96
     trips = slots // step
 
     def products(q, start, stop):

time: 63.2 us -> 62.5 us (0.989)
  Pallas kernels: 61.8 us -> 61 us
    pallas_call x1, Pallas kernels: 60.1 us -> 59.3 us  [local(): pl.pallas_call(functools.partial(kernel, total_rows), out_shape=(pltpu.VM...]
where the time goes in v6:
time: 62.5 us; the launch traced here: 62.3 us
  Pallas kernels  61 us (98%)
  between operations  1.29 us (2%)
    pallas_call x1, Pallas kernels, local(): pl.pallas_call(functools.partial(kernel, total_rows), out_shape=(pltpu.VM...  59.3 us
    pallas_call x1, Pallas kernels, local(): pl.pallas_call(finish, out_shape=(jax.ShapeDtypeStruct((rhs, seg), F32),...  1.72 us

profile of v6, /device:TPU:1, one launch (start us, length us, event | category | flops | bytes accessed | tf_op | source)
XLA Modules:
  0.0 62.3 jit_solution(11551066796570234076)
XLA Ops:
  1.3 59.3 %step.1 = (f32[16,8192]{1,0:T(8,128)S(1)}, bf16[256,8192]{1,0:T(8,128)(2,1)S(1)}, bf16[32,384]{1,0:T(8,128)(2,1)S(1)}, f32[128,16]{1,0:T(8,128)S(1)}, f32[16,16]{1,0:T(8,128)S(1)}) custom-call(s32[1,1]{1,0:T(1,128)S(6)} %copy.9.count_hbm, s32[1,1,384]{2,1,0:T(1,128)} %cols_hbm.1, s32[1,384]{1,0:T(1,128)} %bitcast.6, f32[8,16,8192]{2,1,0:T(8,128)} %basis_hbm.1, ...), custom_call_target="tpu_custom_call" | custom-call | tf_op jit(solution)/shard_map/step/pallas_call | solution.py:602
  60.6 1.7 %finish.1 = (f32[16,8192]{1,0:T(8,128)}, f32[128,16]{1,0:T(8,128)}, f32[16,16]{1,0:T(8,128)}) custom-call(f32[16,8192]{1,0:T(8,128)S(1)} %get-tuple-element.11.w, bf16[256,8192]{1,0:T(8,128)(2,1)S(1)} %get-tuple-element.12.q2, bf16[32,384]{1,0:T(8,128)(2,1)S(1)} %get-tuple-element.13.pairs, f32[128,16]{1,0:T(8,128)S(1)} %get-tuple-element.14.coef, ...), custom_call_target="tpu_custom_call" | custom-call | tf_op jit(solution)/shard_map/finish/pallas_call | solution.py:654
